TPU v7x, 32 devices: a whole 2x2x4 slice. The times are simulated.
32 devices in a mesh: rep: 4 (over z), exp: 8 (over y, x, core).
Axes of the slice: x: 2, y: 2, z: 4, core: 2. Of those that a mesh axis runs over, the one named last changes fastest.
Arguments:
- tokens: bfloat16 [64, 128, 512], P('rep', 'exp'), may hold values from -48 to 48
- gate: float32 [64, 128], P('rep', 'exp'), may hold values from 0.25 to 1
- route: int32 [4, 8, 256, 1], P('rep', 'exp'), may hold values from 0 to 7; in each aligned block of 256 rows (0 to 255, 256 to 511, ..., all dimensions but the last counted through in order) at most 48 rows name the same one
- cotangent: bfloat16 [64, 128, 512], P('rep', 'exp'), may hold values from -6 to 6
- w_qkv: bfloat16 [512, 1536], replicated, may hold values from -1 to 1
- w_proj: bfloat16 [512, 512], replicated, may hold values from -0.25 to 0.25
- w_up: bfloat16 [8, 2048, 512], P('exp', 'rep'), may hold values from -0.25 to 0.25
- w_down: bfloat16 [8, 2048, 512], P('exp', 'rep'), may hold values from -0.125 to 0.125
Outputs:
- layer_out: bfloat16 [64, 128, 512], P('rep', 'exp')
- input_grad: bfloat16 [64, 128, 512], P('rep', 'exp')
- grad_up: float32 [8, 2048, 512], P('exp', 'rep')
- grad_down: float32 [8, 2048, 512], P('exp', 'rep')
Inputs may be any that keep to these rules, and one draw needn't show every extreme that they name: `route`: among the tokens of one tile no expert is named more than 48 times.
All inputs are finite; a program needn't handle non-finite values.
Results may differ from a plain program's by a relative error of at most 0.018.
Values may be sent and summed in bfloat16 or wider, within the bound.
A program may use at most 64 MiB of HBM per device.

v0:
```python
import math

import jax
import jax.numpy as jnp
import numpy as np
from jax import lax
from jax.experimental import pallas as pl
from jax.experimental.pallas import tpu as pltpu
from jax.sharding import PartitionSpec as P

HEADS = 16


GELU_C = math.sqrt(2.0 / math.pi)
window_side = 8
margin_cells = 4


def padded(block, sides, width):
    for axis, dim in sides:
        count = lax.axis_size(axis)
        forward = [(i, i + 1) for i in range(count - 1)]
        backward = [(target, source) for source, target in forward]
        low = lax.ppermute(
            lax.slice_in_dim(block, block.shape[dim] - width, None, axis=dim), axis, forward
        )
        high = lax.ppermute(lax.slice_in_dim(block, 0, width, axis=dim), axis, backward)
        block = jnp.concatenate([low, block, high], axis=dim)
    return block


def gelu_tanh(inputs):
    return 0.5 * inputs * (1.0 + jnp.tanh(GELU_C * (inputs + 0.044715 * inputs * inputs * inputs)))


def gelu_slope(inputs):
    inner = jnp.tanh(GELU_C * (inputs + 0.044715 * inputs * inputs * inputs))
    return 0.5 * (1.0 + inner) + 0.5 * inputs * (1.0 - inner * inner) * GELU_C * (
        1.0 + 3.0 * 0.044715 * inputs * inputs
    )


def layer_norm(values):
    average = jnp.mean(values, axis=-1, keepdims=True)
    centred = values - average
    spread = jnp.mean(centred * centred, axis=-1, keepdims=True)
    return centred * lax.rsqrt(spread + 1e-05)


def window_order(tile_rows, tile_cols):
    wins = (tile_cols + 2 * margin_cells) // window_side
    rows = (np.arange(tile_rows) + margin_cells) // window_side
    cols = (np.arange(tile_cols) + margin_cells) // window_side
    window = (rows[:, None] * wins + cols[None, :]).reshape(-1)
    order = np.argsort(window, kind="stable")
    counts = np.bincount(window)
    return order, tuple((int(c.sum()), int(n)) for c, n in ((counts[:i], counts[i]) for i in range(len(counts))))


def attend_window(number, first, amount, queries, keys_values, absent, context):
    feature = queries.shape[1]
    head_size = feature // HEADS
    cells = window_side * window_side
    group = 128 // head_size
    mine = pl.ds(first, amount)
    theirs = pl.ds(number * cells, cells)
    lane = lax.broadcasted_iota(jnp.int32, (amount, 128), 1)
    keep = [
        ((lane >= h * head_size) & (lane < (h + 1) * head_size)).astype(jnp.float32)
        for h in range(group)
    ]
    for start in range(0, feature, 128):
        query = queries[mine, pl.ds(start, 128)]
        stacked = jnp.concatenate([query * k.astype(jnp.bfloat16) for k in keep], axis=0)
        scores = lax.dot_general(
            stacked,
            keys_values[theirs, pl.ds(start, 128)],
            (((1,), (1,)), ((), ())),
            preferred_element_type=jnp.float32,
        ) / math.sqrt(head_size)
        scores = scores + absent[pl.ds(number, 1), :]
        weights = jnp.exp(scores - jnp.max(scores, axis=-1, keepdims=True))
        total = jnp.sum(weights, axis=-1, keepdims=True)
        probabilities = (weights * (1.0 / total)).astype(jnp.bfloat16)
        mixed = jnp.dot(
            probabilities,
            keys_values[theirs, pl.ds(feature + start, 128)],
            preferred_element_type=jnp.float32,
        )
        picked = sum(k * mixed[h * amount : (h + 1) * amount] for h, k in enumerate(keep))
        context[mine, pl.ds(start, 128)] = picked.astype(jnp.bfloat16)


def enter(ring, ranks):
    barrier = pltpu.get_barrier_semaphore()
    me, row = lax.axis_index("exp"), lax.axis_index("rep")

    def greet(step, carry):
        pl.semaphore_signal(barrier, device_id={"exp": lax.rem(me + step, ring)})
        return carry

    lax.fori_loop(1, ring, greet, 0)

    @pl.when(row > 0)
    def _():
        pl.semaphore_signal(barrier, device_id={"rep": row - 1})

    @pl.when(row < ranks - 1)
    def _():
        pl.semaphore_signal(barrier, device_id={"rep": row + 1})

    below = (row + ranks - 1) // ranks
    above = (2 * ranks - 2 - row) // ranks
    pl.semaphore_wait(barrier, ring - 1 + below + above)


def swap_start(ring, cap, source, target, send_sem, recv_sem):
    me = lax.axis_index("exp")
    mine = pl.ds(pl.multiple_of(me * cap, 16), cap)

    def send(step, carry):
        peer = lax.rem(me + step, ring)
        pltpu.make_async_remote_copy(
            src_ref=source.at[pl.ds(pl.multiple_of(peer * cap, 16), cap)],
            dst_ref=target.at[mine],
            send_sem=send_sem,
            recv_sem=recv_sem,
            device_id={"exp": peer},
        ).start()
        return carry

    lax.fori_loop(1, ring, send, 0)
    pltpu.make_async_copy(source.at[mine], target.at[mine], recv_sem).start()


def await_bytes(ref, sem):
    pltpu.make_async_copy(ref, ref, sem).wait()


def spread_kernel(
    windows, ring, ranks, cap,
    upstream, tokens, extended, absent, marks, order, back_order, w_qkv, w_proj,
    out, placers, mixed,
    held, slots, known, queries, keys_values, context,
    z_send, z_recv, m_send, m_recv, a_send, a_recv,
):
    row = lax.axis_index("rep")
    feature = tokens.shape[1]
    enter(ring, ranks)

    def pass_marks(origin, source, side):
        pltpu.make_async_remote_copy(
            src_ref=source,
            dst_ref=known.at[origin],
            send_sem=m_send.at[origin, (side + 1) // 2],
            recv_sem=m_recv.at[origin],
            device_id={"rep": row + side},
        ).start()

    def pass_on(t, origin, source, side):
        pltpu.make_async_remote_copy(
            src_ref=source,
            dst_ref=held.at[t, origin],
            send_sem=z_send.at[t, origin, (side + 1) // 2],
            recv_sem=z_recv.at[t, origin],
            device_id={"rep": row + side},
        ).start()

    def make_placer(origin, ids):
        slot_ids = lax.broadcasted_iota(jnp.int32, placers.shape[1:], 0)
        placers[origin] = (slot_ids == ids).astype(jnp.float32).astype(jnp.bfloat16)

    def dispatch(t, origin, values):
        slots[t, origin] = jnp.dot(
            placers[origin], values, preferred_element_type=jnp.float32
        ).astype(jnp.bfloat16)
        swap_start(
            ring, cap, slots.at[t, origin], out.at[t, origin], a_send.at[t, origin], a_recv.at[t, origin]
        )

    def own(t, source):
        @pl.when(row < ranks - 1)
        def _():
            if t == 0:
                pass_marks(row, marks, 1)
            pass_on(t, row, source, 1)

        @pl.when(row > 0)
        def _():
            if t == 0:
                pass_marks(row, marks, -1)
            pass_on(t, row, source, -1)

        if t == 0:
            make_placer(row, marks[0:1, :])
        dispatch(t, row, source[...])

    def steps(t, begin, end):
        def step(k, carry):
            for side in (1, -1):
                origin = row - side * k

                @pl.when((origin >= 0) & (origin < ranks))
                def _():
                    onward = row + side
                    inner = (onward >= 0) & (onward < ranks)
                    if t == 0:
                        await_bytes(known.at[origin], m_recv.at[origin])

                        @pl.when(inner)
                        def _():
                            pass_marks(origin, known.at[origin], side)

                    await_bytes(held.at[t, origin], z_recv.at[t, origin])

                    @pl.when(inner)
                    def _():
                        pass_on(t, origin, held.at[t, origin], side)

                    if t == 0:
                        make_placer(origin, known[origin, 0:1, :])
                    dispatch(t, origin, held[t, origin])

            return carry

        lax.fori_loop(begin, end, step, 0)

    own(0, upstream)
    keys_values[...] = jnp.dot(
        extended[...], w_qkv[:, feature:], preferred_element_type=jnp.float32
    ).astype(jnp.bfloat16)
    grouped = jnp.dot(order[...], tokens[...], preferred_element_type=jnp.float32)
    queries[...] = jnp.dot(
        grouped.astype(jnp.bfloat16), w_qkv[:, :feature], preferred_element_type=jnp.float32
    ).astype(jnp.bfloat16)
    rounds = 3
    for part in range(rounds):
        low, high = (len(windows) * p // rounds for p in (part, part + 1))
        for number in range(low, high):
            attend_window(number, *windows[number], queries, keys_values, absent, context)
        begin, end = (1 + (ranks - 1) * p // rounds for p in (part, part + 1))
        if part < rounds - 1 and begin < end:
            steps(0, begin, end)
    ungrouped = jnp.dot(back_order[...], context[...], preferred_element_type=jnp.float32)
    attended = jnp.dot(
        ungrouped.astype(jnp.bfloat16), w_proj[...], preferred_element_type=jnp.float32
    )
    mixed[...] = (tokens[...].astype(jnp.float32) + layer_norm(attended)).astype(jnp.bfloat16)
    own(1, mixed)
    steps(0, 1 + (ranks - 1) * (rounds - 1) // rounds, ranks)
    steps(1, 1, ranks)

    def finish(origin, carry):
        for t in range(2):
            await_bytes(out.at[t, origin], a_recv.at[t, origin])
            sent = slots.at[t, origin, pl.ds(0, (ring - 1) * cap)]
            await_bytes(sent, a_send.at[t, origin])

            @pl.when((origin <= row) & (row < ranks - 1))
            def _():
                await_bytes(held.at[t, origin], z_send.at[t, origin, 1])
                if t == 0:
                    await_bytes(known.at[origin], m_send.at[origin, 1])

            @pl.when((origin >= row) & (row > 0))
            def _():
                await_bytes(held.at[t, origin], z_send.at[t, origin, 0])
                if t == 0:
                    await_bytes(known.at[origin], m_send.at[origin, 0])

        return carry

    lax.fori_loop(0, ranks, finish, 0)


def collect_kernel(
    count, ring, ranks, cap, parts, placers, out, back, sums, z_send, z_recv, a_send, a_recv
):
    row = lax.axis_index("rep")
    enter(ring, ranks)

    def launch(t, target):
        swap_start(
            ring, cap, parts[t].at[target], back.at[t, target], a_send.at[t, target], a_recv.at[t, target]
        )

    def ahead(step, carry):
        k = ranks - step
        for t in range(count):
            for side in (1, -1):
                target = row + side * k

                @pl.when((target >= 0) & (target < ranks))
                def _():
                    launch(t, target)

        return carry

    lax.fori_loop(1, ranks, ahead, 0)
    for t in range(count):
        launch(t, row)

    def placed(t, target):
        await_bytes(back.at[t, target], a_recv.at[t, target])
        return lax.dot_general(
            placers[target],
            back[t, target],
            (((0,), (0,)), ((), ())),
            preferred_element_type=jnp.float32,
        )

    def step(index, carry):
        k = ranks - index
        for t in range(count):
            for side in (1, -1):
                target = row + side * k

                @pl.when((target >= 0) & (target < ranks))
                def _():
                    own = placed(t, target)
                    behind = row - side
                    first = (behind < 0) | (behind >= ranks)

                    @pl.when(first)
                    def _():
                        sums[t, target] = own.astype(jnp.bfloat16)

                    @pl.when(jnp.logical_not(first))
                    def _():
                        await_bytes(sums.at[t, target], z_recv.at[t, target])
                        total = own + sums[t, target].astype(jnp.float32)
                        sums[t, target] = total.astype(jnp.bfloat16)

                    final = ranks if side < 0 else target
                    place = jnp.where(k == 1, final, target)
                    pltpu.make_async_remote_copy(
                        src_ref=sums.at[t, target],
                        dst_ref=sums.at[t, place],
                        send_sem=z_send.at[t, target],
                        recv_sem=z_recv.at[t, place],
                        device_id={"rep": row + side},
                    ).start()

        return carry

    lax.fori_loop(1, ranks, step, 0)
    for t in range(count):
        out[t] = placed(t, row)

        @pl.when(row > 0)
        def _():
            await_bytes(sums.at[t, row], z_recv.at[t, row])
            out[t] += sums[t, row].astype(jnp.float32)

        @pl.when(row < ranks - 1)
        def _():
            await_bytes(sums.at[t, ranks], z_recv.at[t, ranks])
            out[t] += sums[t, ranks].astype(jnp.float32)

    def finish(target, carry):
        for t in range(count):
            sent = back.at[t, target, pl.ds(0, (ring - 1) * cap)]
            await_bytes(sent, a_send.at[t, target])

            @pl.when(target != row)
            def _():
                await_bytes(sums.at[t, target], z_send.at[t, target])

        return carry

    lax.fori_loop(0, ranks, finish, 0)


def in_vmem(amount):
    return [pl.BlockSpec(memory_space=pltpu.VMEM)] * amount


def spread(operands, windows, ring, ranks, cap):
    tok, feature = operands[1].shape
    ext_count = operands[2].shape[0]
    rows = ring * cap

    def body(*refs):
        spread_kernel(windows, ring, ranks, cap, *refs)

    return pl.pallas_call(
        body,
        name="spread",
        out_shape=(
            jax.ShapeDtypeStruct((2, ranks, rows, feature), jnp.bfloat16),
            jax.ShapeDtypeStruct((ranks, rows, tok), jnp.bfloat16),
            jax.ShapeDtypeStruct((tok, feature), jnp.bfloat16),
        ),
        in_specs=in_vmem(len(operands)),
        out_specs=tuple(in_vmem(3)),
        scratch_shapes=[
            pltpu.VMEM((2, ranks, tok, feature), jnp.bfloat16),
            pltpu.VMEM((2, ranks, rows, feature), jnp.bfloat16),
            pltpu.VMEM((ranks, 8, tok), jnp.int32),
            pltpu.VMEM((tok, feature), jnp.bfloat16),
            pltpu.VMEM((ext_count, 2 * feature), jnp.bfloat16),
            pltpu.VMEM((tok, feature), jnp.bfloat16),
            pltpu.SemaphoreType.DMA((2, ranks, 2)),
            pltpu.SemaphoreType.DMA((2, ranks)),
            pltpu.SemaphoreType.DMA((ranks, 2)),
            pltpu.SemaphoreType.DMA((ranks,)),
            pltpu.SemaphoreType.DMA((2, ranks)),
            pltpu.SemaphoreType.DMA((2, ranks)),
        ],
        compiler_params=pltpu.CompilerParams(
            collective_id=0, has_side_effects=True, vmem_limit_bytes=60 << 20
        ),
    )(*operands)


def collect(parts, placers, ring, ranks, cap):
    count = len(parts)
    rows, feature = parts[0].shape[1:]
    tok = placers.shape[2]

    def body(*refs):
        collect_kernel(count, ring, ranks, cap, refs[:count], *refs[count:])

    return pl.pallas_call(
        body,
        name="collect",
        out_shape=jax.ShapeDtypeStruct((count, tok, feature), jnp.float32),
        in_specs=in_vmem(count + 1),
        out_specs=pl.BlockSpec(memory_space=pltpu.VMEM),
        scratch_shapes=[
            pltpu.VMEM((count, ranks, rows, feature), jnp.bfloat16),
            pltpu.VMEM((count, ranks + 1, tok, feature), jnp.bfloat16),
            pltpu.SemaphoreType.DMA((count, ranks)),
            pltpu.SemaphoreType.DMA((count, ranks + 1)),
            pltpu.SemaphoreType.DMA((count, ranks)),
            pltpu.SemaphoreType.DMA((count, ranks)),
        ],
        compiler_params=pltpu.CompilerParams(
            collective_id=1, has_side_effects=True, vmem_limit_bytes=60 << 20
        ),
    )(*parts, placers)


def per_device(tokens, gate, route, cotangent, w_qkv, w_proj, w_up, w_down):
    tile_rows, tile_cols, feature = tokens.shape
    tok_count = tile_rows * tile_cols
    ext_rows = tile_rows + 2 * margin_cells
    ext_cols = tile_cols + 2 * margin_cells
    extended = padded(tokens, (("rep", 0), ("exp", 1)), 4)
    win_rows, win_cols = ext_rows // window_side, ext_cols // window_side

    def by_window(cells):
        split = cells.reshape(win_rows, window_side, win_cols, window_side, -1)
        return split.transpose(0, 2, 1, 3, 4).reshape(win_rows * win_cols, window_side**2, -1)

    row_ids = (
        lax.axis_index("rep") * tile_rows - margin_cells + jnp.arange(ext_rows, dtype=jnp.int32)
    )
    col_ids = (
        lax.axis_index("exp") * tile_cols - margin_cells + jnp.arange(ext_cols, dtype=jnp.int32)
    )
    row_inside = (row_ids >= 0) & (row_ids < tile_rows * lax.axis_size("rep"))
    col_inside = (col_ids >= 0) & (col_ids < tile_cols * lax.axis_size("exp"))
    in_grid = row_inside[:, None] & col_inside[None, :]
    absent = jnp.where(by_window(in_grid)[..., 0], 0.0, -1e30).astype(jnp.float32)
    flat_tokens = tokens.reshape(tok_count, feature)
    order, windows = window_order(tile_rows, tile_cols)
    grouping = np.zeros((tok_count, tok_count), np.float32)
    grouping[np.arange(tok_count), order] = 1.0
    grouping = jnp.asarray(grouping, jnp.bfloat16)
    experts = lax.axis_size("exp")
    ranks = lax.axis_size("rep")
    capacity = max(2, 3 * tok_count // (2 * experts))
    capacity = -(-capacity // 16) * 16
    slot_count = experts * capacity
    chosen = route.reshape(tok_count)
    matches = (chosen[:, None] == jnp.arange(experts, dtype=jnp.int32)[None, :]).astype(jnp.int32)
    position = jnp.sum(matches * (jnp.cumsum(matches, axis=0) - 1), axis=1)
    marks = jnp.broadcast_to((chosen * capacity + position)[None, :], (8, tok_count))
    gate_rows = gate.reshape(tok_count)
    upstream = (
        gate_rows[:, None] * cotangent.reshape(tok_count, feature).astype(jnp.float32)
    ).astype(jnp.bfloat16)
    operands = (
        upstream,
        flat_tokens,
        by_window(extended).reshape(-1, feature),
        absent,
        marks,
        grouping,
        grouping.T,
        w_qkv,
        w_proj,
    )
    gathered, placers, mixed = spread(operands, windows, experts, ranks, capacity)
    slot_grads = gathered[0].reshape(-1, feature)
    slot_rows = gathered[1].reshape(-1, feature)
    up_mat = w_up[0]
    down_mat = w_down[0]
    pre_act = lax.dot_general(
        slot_rows, up_mat, (((1,), (1,)), ((), ())), preferred_element_type=jnp.float32
    )
    hidden = gelu_tanh(pre_act).astype(jnp.bfloat16)
    expert_out = jnp.dot(hidden, down_mat, preferred_element_type=jnp.float32).astype(jnp.bfloat16)
    hidden_grad = lax.dot_general(
        slot_grads, down_mat, (((1,), (1,)), ((), ())), preferred_element_type=jnp.float32
    )
    pre_grad = (hidden_grad * gelu_slope(pre_act)).astype(jnp.bfloat16)
    input_slots = jnp.dot(pre_grad, up_mat, preferred_element_type=jnp.float32).astype(jnp.bfloat16)
    shape = (ranks, slot_count, feature)
    returned = collect(
        (expert_out.reshape(shape), input_slots.reshape(shape)), placers, experts, ranks, capacity
    )
    layer_out = (mixed.astype(jnp.float32) + gate_rows[:, None] * returned[0]).astype(jnp.bfloat16)
    input_grad = returned[1].astype(jnp.bfloat16)
    average_factor = 1.0 / ranks
    grad_up = lax.dot_general(
        pre_grad, slot_rows, (((0,), (0,)), ((), ())), preferred_element_type=jnp.float32
    )
    grad_down = lax.dot_general(
        hidden, slot_grads, (((0,), (0,)), ((), ())), preferred_element_type=jnp.float32
    )
    return (
        layer_out.reshape(tile_rows, tile_cols, feature),
        input_grad.reshape(tile_rows, tile_cols, feature),
        (grad_up * average_factor)[None],
        (grad_down * average_factor)[None],
    )


def solution(mesh):
    placed = (
        P("rep", "exp", None),
        P("rep", "exp"),
        P("rep", "exp", None, None),
        P("rep", "exp", None),
        P(),
        P(),
        P("exp", "rep", None),
        P("exp", "rep", None),
    )
    return jax.shard_map(
        per_device,
        mesh=mesh,
        in_specs=placed,
        out_specs=(
            P("rep", "exp", None),
            P("rep", "exp", None),
            P("exp", "rep", None),
            P("exp", "rep", None),
        ),
        check_vma=False,
    )
```

profile of v0, /device:TPU:7, one launch (start us, length us, event | category | flops | bytes accessed | tf_op | source)
XLA Modules:
  0.0 139.8 jit_solution(14513694470177304254)
XLA Ops:
  0.6 0.0 copy-start
  0.6 0.9 fusion.28
  1.6 1.3 collective-permute-start.1
  2.9 4.0 %collective-permute-start = (bf16[4,16,512]{2,1,0:T(8,128)(2,1)S(1)}, bf16[4,16,512]{2,1,0:T(8,128)(2,1)S(1)}, u32[]{:S(2)}, u32[]{:S(2)}) collective-permute-start(bf16[4,16,512]{2,1,0:T(8,128)(2,1)S(1)} %get-tuple-element.15), channel_id=1, source_target_pairs={{0,8},{8,16},{16,24},{1,9},{9,17},{17,25},{2,10},{10,18},{18,26},{... | collective-permute-start | bytes 196616 | tf_op jit(solution)/shard_map/ppermute | solution.py:24
  6.9 0.8 mul.91
  7.7 0.7 fusion.17
  8.4 0.6 reduce-window.6
  8.9 0.2 slice_reduce_fusion
  9.2 0.1 select_bitcast_fusion
  9.3 1.8 %fusion.8.refs_0_ = bf16[256,512]{1,0:T(8,128)(2,1)} fusion(bf16[16,16,512]{2,1,0:T(8,128)(2,1)} %param.12, f32[256]{0:T(256)S(1)} %mul.91), kind=kLoop, calls=%fused_computation.19 | loop fusion | flops 393216 | bytes 525312 | tf_op jit(solution)/shard_map/convert_element_type | solution.py:483
  11.0 0.8 fusion.16
  11.8 0.0 collective-permute-done
  11.8 1.0 constant_dynamic-update-slice_fusion.1
  12.8 0.0 collective-permute-done.1
  12.8 0.1 fusion.27
  12.9 1.3 collective-permute-start.2
  14.2 3.8 %collective-permute-start.3 = (bf16[24,4,512]{2,1,0:T(4,128)(2,1)S(1)}, bf16[24,4,512]{2,1,0:T(4,128)(2,1)S(1)}, u32[]{:S(2)}, u32[]{:S(2)}) collective-permute-start(bf16[24,4,512]{2,1,0:T(4,128)(2,1)S(1)} %get-tuple-element.13), channel_id=1, source_target_pairs={{1,0},{2,1},{3,2},{4,3},{5,4},{6,5},{7,6},{9,8},{10,9},{11,10},{12... | collective-permute-start | bytes 294920 | tf_op jit(solution)/shard_map/ppermute | solution.py:27
  18.0 0.7 multiply_add_fusion.2
  18.7 0.7 select_n.10.refs_3_
  19.4 0.0 collective-permute-done.2
  19.4 0.0 collective-permute-done.3
  19.4 0.3 pad_maximum_fusion
  19.7 0.9 copy.14
  20.6 0.6 broadcast_in_dim.25.refs_4_
  21.2 54.6 %spread.1 = (bf16[2,4,384,512]{3,2,1,0:T(8,128)(2,1)}, bf16[4,384,256]{2,1,0:T(8,128)(2,1)}, bf16[256,512]{1,0:T(8,128)(2,1)}) custom-call(bf16[256,512]{1,0:T(8,128)(2,1)} %fusion.8.refs_0_, bf16[256,512]{1,0:T(8,128)(2,1)} %bitcast.58, bf16[576,512]{1,0:T(8,128)(2,1)} %bitcast.57, f32[9,64]{1,0:T(8,128)} %select_n.10.refs_3_, ...), custom_call_target="tpu_custom_call" | custom-call | tf_op jit(solution)/shard_map/spread/pallas_call | solution.py:386
  75.7 0.0 copy-start.1
  75.7 2.1 %fusion.26 = (bf16[1,4,384,512]{3,2,1,0:T(8,128)(2,1)S(1)}, bf16[1,4,384,512]{3,2,1,0:T(8,128)(2,1)S(1)}) fusion(bf16[2,4,384,512]{3,2,1,0:T(8,128)(2,1)} %get-tuple-element.8), kind=kLoop, calls=%fused_computation.48 | loop fusion | bytes 6291456 | tf_op jit(solution)/shard_map/slice | solution.py:496
  77.9 0.0 copy-done.1
  77.9 1.0 fusion.14
  78.9 2.3 %fusion.6 = f32[1,512,512]{2,1,0:T(8,128)} fusion(bf16[1536,512]{1,0:T(8,128)(2,1)S(1)} %bitcast.61, f32[1536,512]{1,0:T(8,128)S(1)} %fusion.14), kind=kOutput, calls=%fused_computation.13 | convolution fusion | flops 812646400 | bytes 5767168 | tf_op jit(solution)/shard_map/dot_general | solution.py:520
  81.3 0.0 copy-done
  81.3 2.4 %fusion.5 = bf16[1536,512]{1,0:T(8,128)(2,1)S(1)} fusion(f32[1536,512]{1,0:T(8,128)S(1)} %fusion.14, bf16[1536,512]{1,0:T(8,128)(2,1)S(1)} %bitcast.62, bf16[1,512,512]{2,1,0:T(8,128)(2,1)S(1)} %copy-done), kind=kOutput, calls=%fused_computation.11 | convolution fusion | flops 820248576 | bytes 6815744 | tf_op jit(solution)/shard_map/dot_general | solution.py:505
  83.7 2.4 %convolution_convert_fusion.1 = bf16[1536,512]{1,0:T(8,128)(2,1)} fusion(bf16[1,512,512]{2,1,0:T(8,128)(2,1)S(1)} %copy-done, f32[1536,512]{1,0:T(8,128)S(1)} %fusion.14), kind=kOutput, calls=%fused_computation.10 | convolution fusion | flops 813170688 | bytes 5242880 | tf_op jit(solution)/shard_map/dot_general | solution.py:504
  86.1 2.0 %fusion.7 = f32[1,512,512]{2,1,0:T(8,128)} fusion(bf16[1536,512]{1,0:T(8,128)(2,1)S(1)} %fusion.5, bf16[1536,512]{1,0:T(8,128)(2,1)S(1)} %bitcast.55), kind=kOutput, calls=%fused_computation.15 | convolution fusion | flops 805568512 | bytes 4194304 | tf_op jit(solution)/shard_map/dot_general | solution.py:517
  88.0 2.1 %convolution_convert_fusion = bf16[1536,512]{1,0:T(8,128)(2,1)} fusion(bf16[1536,512]{1,0:T(8,128)(2,1)S(1)} %fusion.5, bf16[1,512,512]{2,1,0:T(8,128)(2,1)S(1)} %copy-done.1), kind=kOutput, calls=%fused_computation.9 | convolution fusion | flops 806092800 | bytes 3670016 | tf_op jit(solution)/shard_map/dot_general | solution.py:509
  90.2 0.0 copy-start.2
  90.2 46.0 %collect.1 = f32[2,256,512]{2,1,0:T(8,128)} custom-call(bf16[4,384,512]{2,1,0:T(8,128)(2,1)} %bitcast.59, bf16[4,384,512]{2,1,0:T(8,128)(2,1)} %bitcast.60, bf16[4,384,256]{2,1,0:T(8,128)(2,1)} %get-tuple-element.9.refs_2_), custom_call_target="tpu_custom_call" | custom-call | tf_op jit(solution)/shard_map/collect/pallas_call | solution.py:424
  136.1 1.8 %slice.48 = bf16[1,256,512]{2,1,0:T(8,128)(2,1)} slice(f32[2,256,512]{2,1,0:T(8,128)} %collect.1), slice={[1:2], [0:256], [0:512]} | slice | bytes 524288 | tf_op jit(solution)/shard_map/slice | solution.py:515
  137.9 0.0 copy-done.2
  137.9 1.9 %fusion.10 = bf16[256,512]{1,0:T(8,128)(2,1)} fusion(f32[2,256,512]{2,1,0:T(8,128)} %collect.1, bf16[256,512]{1,0:T(8,128)(2,1)S(1)} %copy-done.2, f32[256]{0:T(256)S(1)} %mul.91), kind=kLoop, calls=%fused_computation.22 | loop fusion | flops 524288 | bytes 1049600 | tf_op jit(solution)/shard_map/convert_element_type | solution.py:514
  (5 shorter events, 0.1 us)
Async XLA Ops:
  0.6 80.6 %copy-start = (bf16[1,512,512]{2,1,0:T(8,128)(2,1)S(1)}, bf16[1,512,512]{2,1,0:T(8,128)(2,1)}, u32[]{:S(2)}) copy-start(bf16[1,512,512]{2,1,0:T(8,128)(2,1)} %param.16) | copy-start | bytes 1572868
  1.6 11.2 %collective-permute-start.1 = (bf16[4,16,512]{2,1,0:T(8,128)(2,1)S(1)}, bf16[4,16,512]{2,1,0:T(8,128)(2,1)S(1)}, u32[]{:S(2)}, u32[]{:S(2)}) collective-permute-start(bf16[4,16,512]{2,1,0:T(8,128)(2,1)S(1)} %get-tuple-element.14), channel_id=1, source_target_pairs={{8,0},{16,8},{24,16},{9,1},{17,9},{25,17},{10,2},{18,10},{26,18},{... | collective-permute-start | bytes 196616 | tf_op jit(solution)/shard_map/ppermute | solution.py:27
  2.9 8.9 %collective-permute-start = (bf16[4,16,512]{2,1,0:T(8,128)(2,1)S(1)}, bf16[4,16,512]{2,1,0:T(8,128)(2,1)S(1)}, u32[]{:S(2)}, u32[]{:S(2)}) collective-permute-start(bf16[4,16,512]{2,1,0:T(8,128)(2,1)S(1)} %get-tuple-element.15), channel_id=1, source_target_pairs={{0,8},{8,16},{16,24},{1,9},{9,17},{17,25},{2,10},{10,18},{18,26},{... | collective-permute-start | bytes 196616 | tf_op jit(solution)/shard_map/ppermute | solution.py:24
  12.9 6.5 %collective-permute-start.2 = (bf16[24,4,512]{2,1,0:T(4,128)(2,1)S(1)}, bf16[24,4,512]{2,1,0:T(4,128)(2,1)S(1)}, u32[]{:S(2)}, u32[]{:S(2)}) collective-permute-start(bf16[24,4,512]{2,1,0:T(4,128)(2,1)S(1)} %get-tuple-element.12), channel_id=1, source_target_pairs={{0,1},{1,2},{2,3},{3,4},{4,5},{5,6},{6,7},{8,9},{9,10},{10,11},{11... | collective-permute-start | bytes 294920 | tf_op jit(solution)/shard_map/ppermute | solution.py:24
  14.2 5.2 %collective-permute-start.3 = (bf16[24,4,512]{2,1,0:T(4,128)(2,1)S(1)}, bf16[24,4,512]{2,1,0:T(4,128)(2,1)S(1)}, u32[]{:S(2)}, u32[]{:S(2)}) collective-permute-start(bf16[24,4,512]{2,1,0:T(4,128)(2,1)S(1)} %get-tuple-element.13), channel_id=1, source_target_pairs={{1,0},{2,1},{3,2},{4,3},{5,4},{6,5},{7,6},{9,8},{10,9},{11,10},{12... | collective-permute-start | bytes 294920 | tf_op jit(solution)/shard_map/ppermute | solution.py:27
  75.7 2.2 %copy-start.1 = (bf16[1,512,512]{2,1,0:T(8,128)(2,1)S(1)}, bf16[1,512,512]{2,1,0:T(8,128)(2,1)}, u32[]{:S(2)}) copy-start(bf16[1,512,512]{2,1,0:T(8,128)(2,1)} %param.15) | copy-start | bytes 1572868
  90.2 47.7 %copy-start.2 = (bf16[256,512]{1,0:T(8,128)(2,1)S(1)}, bf16[256,512]{1,0:T(8,128)(2,1)}, u32[]{:S(2)}) copy-start(bf16[256,512]{1,0:T(8,128)(2,1)} %get-tuple-element.7) | copy-start | bytes 786436
where the time goes:
time: 142 us; the launch traced here: 140 us
  Pallas kernels  101 us (71%)
  matrix products  12.3 us (9%)
  starting transfers between devices  10.3 us (7%)
  local copies, waits for them, and re-layouts  9.09 us (6%)
  other arithmetic  6.79 us (5%)
    pallas_call x1, Pallas kernels, spread(): pl.pallas_call(body, name='spread', out_shape=(jax.ShapeDtypeStruct((2, r...  54.6 us
    pallas_call x1, Pallas kernels, collect(): pl.pallas_call(body, name='collect', out_shape=jax.ShapeDtypeStruct((coun...  46 us
    ppermute x2, starting transfers between devices, padded(): lax.ppermute(lax.slice_in_dim(block, block.shape[dim] - width, None, axis...  5.28 us
    ppermute x2, starting transfers between devices, padded(): lax.ppermute(lax.slice_in_dim(block, 0, width, axis=dim), axis, backward)  5.07 us
  transfers between devices with their start and end apart: 4, of which 0 were waited for; matrix products, arithmetic and copies ran while one was open for 5% of the time, Pallas kernels for 0%

commit v1 on v0

v1 whole, which is shorter than its diff:
```python
import math

import jax
import jax.numpy as jnp
import numpy as np
from jax import lax
from jax.experimental import pallas as pl
from jax.experimental.pallas import tpu as pltpu
from jax.sharding import PartitionSpec as P

HEADS = 16
GELU_C = math.sqrt(2.0 / math.pi)
window_side = 8
margin_cells = 4
PAIR = 2
f32, bf16 = jnp.float32, jnp.bfloat16


class Windows:
    def __init__(self, tile_rows, tile_cols):
        def cut(size):
            parts = [margin_cells] + [window_side] * ((size - 2 * margin_cells) // window_side)
            return parts + [margin_cells]

        self.heights, self.widths = cut(tile_rows), cut(tile_cols)
        self.cells = window_side * window_side
        self.wins, start = [], 0
        position = np.zeros((tile_rows, tile_cols), np.int32)
        top = 0
        for i, h in enumerate(self.heights):
            left = 0
            for j, w in enumerate(self.widths):
                position[top : top + h, left : left + w] = start + np.arange(h * w).reshape(h, w)
                sizes = (h * w, (window_side - h) * w, h * (window_side - w), (window_side - h) * (window_side - w))
                self.wins.append((i, j, start, sizes))
                start += h * w
                left += w
            top += h
        self.position = position.reshape(-1)
        self.last = (len(self.heights) - 1, len(self.widths) - 1)

    def number(self, i, j):
        return i * len(self.widths) + j

    def segment(self, number, kind):
        sizes = self.wins[number][3]
        return number * self.cells + sum(sizes[:kind]), sizes[kind]

    def pieces(self, dv, dh):
        found = []
        for number, (i, j, _, _) in enumerate(self.wins):
            vertical = (dv == -1 and i == 0) or (dv == 1 and i == self.last[0])
            beside = (dh == -1 and j == 0) or (dh == 1 and j == self.last[1])
            if (dv and not vertical) or (dh and not beside):
                continue
            kind = (1 if dv else 0) + (2 if dh else 0)
            theirs = self.number(self.last[0] - i if dv else i, self.last[1] - j if dh else j)
            place, rows = self.segment(number, kind)
            found.append((self.wins[theirs][2], place, rows))
        return found


SIDES = [(v, h) for v in (-1, 0, 1) for h in (-1, 0, 1) if (v, h) != (0, 0)]


def each(begin, end, body):
    if end - begin == 1:
        body(begin)
    elif end > begin:
        lax.fori_loop(begin, end, lambda k, carry: (body(k), carry)[1], 0)


def drain(ref, sem):
    pltpu.make_async_copy(ref, ref, sem).wait()


def dot_t(a, b):
    return lax.dot_general(a, b, (((1,), (1,)), ((), ())), preferred_element_type=f32)


def t_dot(a, b):
    return lax.dot_general(a, b, (((0,), (0,)), ((), ())), preferred_element_type=f32)


def dot(a, b):
    return jnp.dot(a, b, preferred_element_type=f32)


def layer_norm(values):
    average = jnp.mean(values, axis=-1, keepdims=True)
    centred = values - average
    spread = jnp.mean(centred * centred, axis=-1, keepdims=True)
    return centred * lax.rsqrt(spread + 1e-05)


def layer_kernel(
    wins, ring, ranks, cap, tile_cols,
    tokens, cotangent, gate, route, position, w_qkv_hbm, w_proj_hbm, w_up_hbm, w_down_hbm,
    layer_out, input_grad, grad_up, grad_down,
    w_qkv, w_proj, w_up, w_down, grouped, ext, kv, queries, context, mixed, upstream, gate_col,
    marks, placers, held, slots, gathered, hidden, pre_grad, parts, back, sums, arrived, share, taken,
    load_sem, halo_send, halo_recv, mark_send, mark_recv, z_send, z_recv, a_send, a_recv,
    b_send, b_recv, w_send, w_recv, r_send, r_recv, g_send, g_recv,
):
    me, row = lax.axis_index("exp"), lax.axis_index("rep")
    tok, feature = tokens.shape
    units = w_up.shape[1]
    tiles = ranks // PAIR
    buddy = row + 1 - 2 * lax.rem(row, 2)
    head_size = feature // HEADS

    def partner(j):
        return lax.rem(row + PAIR * j, ranks)

    loads = [
        pltpu.make_async_copy(source, target, load_sem.at[i])
        for i, (source, target) in enumerate(
            ((w_up_hbm, w_up.at[0]), (w_down_hbm, w_down.at[0]), (w_qkv_hbm, w_qkv), (w_proj_hbm, w_proj))
        )
    ]
    for load in loads:
        load.start()

    barrier = pltpu.get_barrier_semaphore()

    def near(v, h):
        conds = []
        if v:
            conds.append((row + v >= 0) & (row + v < ranks))
        if h:
            conds.append((me + h >= 0) & (me + h < ring))
        return conds[0] if len(conds) == 1 else conds[0] & conds[1]

    def greet_ring(step, carry):
        pl.semaphore_signal(barrier, device_id={"exp": lax.rem(me + step, ring)})
        return carry

    def greet_ranks(step, carry):
        pl.semaphore_signal(barrier, device_id={"rep": lax.rem(row + step, ranks)})
        return carry

    lax.fori_loop(1, ring, greet_ring, 0)
    lax.fori_loop(1, ranks, greet_ranks, 0)
    for v, h in SIDES:
        if v and h:
            @pl.when(near(v, h))
            def _():
                pl.semaphore_signal(barrier, device_id={"rep": row + v, "exp": me + h})

    spots = position[0:1, :]
    perm = (lax.broadcasted_iota(jnp.int32, (tok, tok), 0) == spots).astype(f32).astype(bf16)
    grouped[...] = dot(perm, tokens[...]).astype(bf16)
    for number, (i, j, start, sizes) in enumerate(wins.wins):
        ext[pl.ds(number * wins.cells, sizes[0]), :] = grouped[pl.ds(start, sizes[0]), :]
    for v, h in SIDES:
        @pl.when(jnp.logical_not(near(v, h)))
        def _():
            for _, place, rows in wins.pieces(v, h):
                ext[pl.ds(place, rows), :] = jnp.zeros((rows, feature), bf16)

    down = (row + ranks - 1) // ranks + (2 * ranks - 2 - row) // ranks
    across = (me + ring - 1) // ring + (2 * ring - 2 - me) // ring
    pl.semaphore_wait(barrier, ring - 1 + ranks - 1 + down * across)

    for index, (v, h) in enumerate(SIDES):
        @pl.when(near(v, h))
        def _():
            device = {"rep": row + v} if not h else {"exp": me + h} if not v else {"rep": row + v, "exp": me + h}
            for source, place, rows in wins.pieces(-v, -h):
                pltpu.make_async_remote_copy(
                    src_ref=grouped.at[pl.ds(source, rows)],
                    dst_ref=ext.at[pl.ds(place, rows)],
                    send_sem=halo_send.at[index],
                    recv_sem=halo_recv.at[len(SIDES) - 1 - index],
                    device_id=device,
                ).start()

    lanes = max(8, ring)
    routes = route[0:1, :].astype(f32)
    match = (lax.broadcasted_iota(jnp.int32, (lanes, tok), 0).astype(f32) == routes).astype(f32)
    before = (
        lax.broadcasted_iota(jnp.int32, (tok, tok), 0) < lax.broadcasted_iota(jnp.int32, (tok, tok), 1)
    ).astype(f32).astype(bf16)
    earlier = dot(match.astype(bf16), before)
    ids = routes * cap + jnp.sum(match * earlier, axis=0, keepdims=True)
    marks[0] = jnp.broadcast_to(ids.astype(jnp.int32), marks.shape[1:])

    def send_marks(j):
        pltpu.make_async_remote_copy(
            src_ref=marks.at[0],
            dst_ref=marks.at[tiles - j],
            send_sem=mark_send.at[j],
            recv_sem=mark_recv.at[tiles - j],
            device_id={"rep": partner(j)},
        ).start()

    def send_tokens(t, source, j):
        pltpu.make_async_remote_copy(
            src_ref=source,
            dst_ref=held.at[t, tiles - j],
            send_sem=z_send.at[t, j],
            recv_sem=z_recv.at[t, tiles - j],
            device_id={"rep": partner(j)},
        ).start()

    def make_placer(j):
        slot_ids = lax.broadcasted_iota(jnp.int32, placers.shape[1:], 0)
        placers[j] = (slot_ids == marks[j, 0:1, :]).astype(f32).astype(bf16)

    def swap(source, target, send_sem, recv_sem):
        mine = pl.ds(pl.multiple_of(me * cap, 16), cap)

        def send(step, carry):
            peer = lax.rem(me + step, ring)
            pltpu.make_async_remote_copy(
                src_ref=source.at[pl.ds(pl.multiple_of(peer * cap, 16), cap)],
                dst_ref=target.at[mine],
                send_sem=send_sem,
                recv_sem=recv_sem,
                device_id={"exp": peer},
            ).start()
            return carry

        lax.fori_loop(1, ring, send, 0)
        pltpu.make_async_copy(source.at[mine], target.at[mine], recv_sem).start()

    def dispatch(t, j, values):
        slots[t, j] = dot(placers[j], values).astype(bf16)
        swap(slots.at[t, j], gathered.at[t, j], a_send.at[t, j], a_recv.at[t, j])

    each(1, tiles, send_marks)
    grid_row = lax.broadcasted_iota(jnp.int32, (tok, gate.shape[0]), 0) // tile_cols
    picks = (grid_row == lax.broadcasted_iota(jnp.int32, (tok, gate.shape[0]), 1)).astype(f32)
    gate_rows = lax.dot_general(
        picks, gate[...], (((1,), (0,)), ((), ())), precision=lax.Precision.HIGHEST, preferred_element_type=f32
    )
    grid_col = lax.rem(lax.broadcasted_iota(jnp.int32, (tok, tile_cols), 0), tile_cols)
    chosen = jnp.where(grid_col == lax.broadcasted_iota(jnp.int32, (tok, tile_cols), 1), gate_rows, 0.0)
    gate_col[...] = jnp.broadcast_to(jnp.sum(chosen, axis=1, keepdims=True), gate_col.shape)
    upstream[...] = (gate_col[:, 0:1] * cotangent[...].astype(f32)).astype(bf16)
    each(1, tiles, lambda j: send_tokens(0, upstream, j))
    make_placer(0)
    dispatch(0, 0, upstream[...])

    def send_weight(index, source, target):
        loads[index].wait()
        pltpu.make_async_remote_copy(
            src_ref=source,
            dst_ref=target,
            send_sem=w_send.at[index],
            recv_sem=w_recv.at[index],
            device_id={"rep": buddy},
        ).start()

    send_weight(0, w_up.at[0], w_up.at[1])
    send_weight(1, w_down.at[0], w_down.at[1])

    loads[2].wait()
    queries[...] = dot(grouped[...], w_qkv[:, :feature]).astype(bf16)
    for index, (v, h) in enumerate(SIDES):
        @pl.when(near(v, h))
        def _():
            amount = sum(rows for _, _, rows in wins.pieces(v, h))
            drain(grouped.at[pl.ds(0, amount)], halo_recv.at[index])

    kv[...] = dot(ext[...], w_qkv[:, feature:]).astype(bf16)
    key_lane = lax.broadcasted_iota(jnp.int32, (1, wins.cells), 1)
    group = 128 // head_size

    def attend(number):
        i, j, start, sizes = wins.wins[number]
        amount = sizes[0]
        absent = jnp.zeros((1, wins.cells), f32)
        v = -1 if i == 0 else 1 if i == wins.last[0] else 0
        h = -1 if j == 0 else 1 if j == wins.last[1] else 0
        for side in {(v, 0), (0, h), (v, h)} - {(0, 0)}:
            kind = (1 if side[0] else 0) + (2 if side[1] else 0)
            first = sum(sizes[:kind])
            inside = (key_lane >= first) & (key_lane < first + sizes[kind])
            missing = jnp.where(near(*side), 0.0, -1e30)
            absent = jnp.where(inside, missing, absent)
        lane = lax.broadcasted_iota(jnp.int32, (amount, 128), 1)
        keep = [((lane >= g * head_size) & (lane < (g + 1) * head_size)).astype(f32) for g in range(group)]
        mine, theirs = pl.ds(start, amount), pl.ds(number * wins.cells, wins.cells)
        for first in range(0, feature, 128):
            query = queries[mine, pl.ds(first, 128)]
            stacked = jnp.concatenate([query * k.astype(bf16) for k in keep], axis=0)
            scores = dot_t(stacked, kv[theirs, pl.ds(first, 128)]) * (1.0 / math.sqrt(head_size)) + absent
            weights = jnp.exp(scores - jnp.max(scores, axis=-1, keepdims=True))
            total = jnp.sum(weights, axis=-1, keepdims=True)
            probs = (weights * (1.0 / total)).astype(bf16)
            found = dot(probs, kv[theirs, pl.ds(feature + first, 128)])
            picked = sum(k * found[g * amount : (g + 1) * amount] for g, k in enumerate(keep))
            context[mine, pl.ds(first, 128)] = picked.astype(bf16)

    def bring(t, j):
        if t == 0:
            drain(marks.at[0], mark_recv.at[j])
            make_placer(j)
        drain(held.at[t, j], z_recv.at[t, j])
        dispatch(t, j, held[t, j])

    count = len(wins.wins)
    for number in range(count // 2):
        attend(number)
    each(1, tiles, lambda j: bring(0, j))
    for number in range(count // 2, count):
        attend(number)

    loads[3].wait()
    attended = dot(context[...], w_proj[...])
    blended = (grouped[...].astype(f32) + layer_norm(attended)).astype(bf16)
    mixed[...] = t_dot(perm, blended).astype(bf16)
    each(1, tiles, lambda j: send_tokens(1, mixed, j))
    dispatch(1, 0, mixed[...])

    def arrive(t, j):
        drain(gathered.at[t, j], a_recv.at[t, j])

    block = min(256, units)

    def experts(j):
        arrive(0, j)
        arrive(1, j)
        for half in range(PAIR):
            for first in range(0, units, block):
                spot = pl.ds(half * units + first, block)
                up, low = w_up[half, pl.ds(first, block), :], w_down[half, pl.ds(first, block), :]
                pre = dot_t(gathered[1, j], up)
                flow = dot_t(gathered[0, j], low)
                square = pre * pre
                inner = jnp.tanh(GELU_C * (pre + 0.044715 * square * pre))
                hidden[j, :, spot] = (0.5 * pre * (1.0 + inner)).astype(bf16)
                slope = 0.5 * (1.0 + inner) + 0.5 * pre * (1.0 - inner * inner) * GELU_C * (
                    1.0 + 3.0 * 0.044715 * square
                )
                pre_grad[j, :, spot] = (flow * slope).astype(bf16)
        for t, (left, right) in enumerate(((hidden, w_down), (pre_grad, w_up))):
            total = dot(left[j, :, pl.ds(0, units)], right[0])
            for half in range(1, PAIR):
                total += dot(left[j, :, pl.ds(half * units, units)], right[half])
            parts[t, j] = total.astype(bf16)
            swap(parts.at[t, j], back.at[t, j], b_send.at[t, j], b_recv.at[t, j])

    for index, weight in enumerate((w_up, w_down)):
        drain(weight.at[1], w_recv.at[index])
    experts(0)
    each(1, tiles, lambda j: bring(1, j))
    each(1, tiles, experts)

    rows = tiles * hidden.shape[1]

    def gradient(t, half):
        left = (pre_grad, hidden)[t][...].reshape(rows, PAIR * units)[:, half * units : (half + 1) * units]
        return t_dot(left, gathered[1 - t].reshape(rows, feature))

    for t in range(2):
        share[t] = gradient(t, 1).astype(bf16)
        pltpu.make_async_remote_copy(
            src_ref=share.at[t],
            dst_ref=taken.at[t],
            send_sem=g_send.at[t],
            recv_sem=g_recv.at[t],
            device_id={"rep": buddy},
        ).start()

    def placed(t, j):
        drain(back.at[t, j], b_recv.at[t, j])
        return t_dot(placers[j], back[t, j])

    def give(j):
        for t in range(2):
            sums[t, j] = placed(t, j).astype(bf16)
            pltpu.make_async_remote_copy(
                src_ref=sums.at[t, j],
                dst_ref=arrived.at[t, tiles - j],
                send_sem=r_send.at[t, j],
                recv_sem=r_recv.at[t, tiles - j],
                device_id={"rep": partner(j)},
            ).start()

    each(1, tiles, give)
    grad_up[...] = gradient(0, 0)
    grad_down[...] = gradient(1, 0)

    def total_of(t):
        value = placed(t, 0)
        for j in range(1, tiles):
            drain(arrived.at[t, j], r_recv.at[t, j])
            value += arrived[t, j].astype(f32)
        return value

    layer_out[...] = (mixed[...].astype(f32) + gate_col[:, 0:1] * total_of(0)).astype(bf16)
    input_grad[...] = total_of(1).astype(bf16)
    factor = 1.0 / ranks
    for t, out in enumerate((grad_up, grad_down)):
        drain(taken.at[t], g_recv.at[t])
        out[...] = (out[...] + taken[t].astype(f32)) * factor

    for index, (v, h) in enumerate(SIDES):
        @pl.when(near(v, h))
        def _():
            amount = sum(rows for _, _, rows in wins.pieces(-v, -h))
            drain(grouped.at[pl.ds(0, amount)], halo_send.at[index])

    for t in range(2):
        drain(w_up.at[0], w_send.at[t])
        drain(share.at[t], g_send.at[t])

    def finish(j):
        for t in range(2):
            sent = slots.at[t, j, pl.ds(0, (ring - 1) * cap)]
            drain(sent, a_send.at[t, j])
            drain(sent, b_send.at[t, j])

    each(0, tiles, finish)

    def finish_far(j):
        drain(marks.at[0], mark_send.at[j])
        for t in range(2):
            drain(mixed, z_send.at[t, j])
            drain(mixed, r_send.at[t, j])

    each(1, tiles, finish_far)


def per_device(ranks, ring, tokens, gate, route, cotangent, w_qkv, w_proj, w_up, w_down):
    tile_rows, tile_cols, feature = tokens.shape
    tok = tile_rows * tile_cols
    units = w_up.shape[1]
    capacity = max(2, 3 * tok // (2 * ring))
    capacity = -(-capacity // 16) * 16
    rows = ring * capacity
    tiles = ranks // PAIR
    wins = Windows(tile_rows, tile_cols)
    ext = len(wins.wins) * wins.cells
    position = jnp.asarray(np.broadcast_to(wins.position[None, :], (8, tok)))

    def body(*refs):
        layer_kernel(wins, ring, ranks, capacity, tile_cols, *refs)

    vmem, anywhere = pl.BlockSpec(memory_space=pltpu.VMEM), pl.BlockSpec(memory_space=pl.ANY)
    dma = pltpu.SemaphoreType.DMA
    layer_out, input_grad, grad_up, grad_down = pl.pallas_call(
        body,
        name="layer",
        out_shape=(
            jax.ShapeDtypeStruct((tok, feature), bf16),
            jax.ShapeDtypeStruct((tok, feature), bf16),
            jax.ShapeDtypeStruct((units, feature), f32),
            jax.ShapeDtypeStruct((units, feature), f32),
        ),
        in_specs=[vmem] * 5 + [anywhere] * 4,
        out_specs=(vmem,) * 4,
        scratch_shapes=[
            pltpu.VMEM(w_qkv.shape, bf16),
            pltpu.VMEM(w_proj.shape, bf16),
            pltpu.VMEM((PAIR, units, feature), bf16),
            pltpu.VMEM((PAIR, units, feature), bf16),
            pltpu.VMEM((tok, feature), bf16),
            pltpu.VMEM((ext, feature), bf16),
            pltpu.VMEM((ext, 2 * feature), bf16),
            pltpu.VMEM((tok, feature), bf16),
            pltpu.VMEM((tok, feature), bf16),
            pltpu.VMEM((tok, feature), bf16),
            pltpu.VMEM((tok, feature), bf16),
            pltpu.VMEM((tok, 128), f32),
            pltpu.VMEM((tiles, 8, tok), jnp.int32),
            pltpu.VMEM((tiles, rows, tok), bf16),
            pltpu.VMEM((2, tiles, tok, feature), bf16),
            pltpu.VMEM((2, tiles, rows, feature), bf16),
            pltpu.VMEM((2, tiles, rows, feature), bf16),
            pltpu.VMEM((tiles, rows, PAIR * units), bf16),
            pltpu.VMEM((tiles, rows, PAIR * units), bf16),
            pltpu.VMEM((2, tiles, rows, feature), bf16),
            pltpu.VMEM((2, tiles, rows, feature), bf16),
            pltpu.VMEM((2, tiles, tok, feature), bf16),
            pltpu.VMEM((2, tiles, tok, feature), bf16),
            pltpu.VMEM((2, units, feature), bf16),
            pltpu.VMEM((2, units, feature), bf16),
            dma((4,)),
            dma((len(SIDES),)),
            dma((len(SIDES),)),
            dma((tiles,)),
            dma((tiles,)),
            dma((2, tiles)),
            dma((2, tiles)),
            dma((2, tiles)),
            dma((2, tiles)),
            dma((2, tiles)),
            dma((2, tiles)),
            dma((2,)),
            dma((2,)),
            dma((2, tiles)),
            dma((2, tiles)),
            dma((2,)),
            dma((2,)),
        ],
        compiler_params=pltpu.CompilerParams(
            collective_id=0, has_side_effects=True, vmem_limit_bytes=60 << 20
        ),
    )(
        tokens.reshape(tok, feature),
        cotangent.reshape(tok, feature),
        gate,
        route.reshape(1, tok),
        position,
        w_qkv,
        w_proj,
        w_up[0],
        w_down[0],
    )
    return (
        layer_out.reshape(tile_rows, tile_cols, feature),
        input_grad.reshape(tile_rows, tile_cols, feature),
        grad_up[None],
        grad_down[None],
    )


def solution(mesh):
    ranks, ring = mesh.shape["rep"], mesh.shape["exp"]
    placed = (
        P("rep", "exp", None),
        P("rep", "exp"),
        P("rep", "exp", None, None),
        P("rep", "exp", None),
        P(),
        P(),
        P("exp", "rep", None),
        P("exp", "rep", None),
    )

    def device(*arrays):
        return per_device(ranks, ring, *arrays)

    return jax.shard_map(
        device,
        mesh=mesh,
        in_specs=placed,
        out_specs=(
            P("rep", "exp", None),
            P("rep", "exp", None),
            P("exp", "rep", None),
            P("exp", "rep", None),
        ),
        check_vma=False,
    )
```

time: 142 us -> 108 us (0.76)
  the two profiles are of different devices: /device:TPU:7 before, /device:TPU:9 now
where the time goes in v1:
time: 108 us
  Pallas kernels  101 us (94%)
  local copies, waits for them, and re-layouts  6.71 us (6%)
    pallas_call x1, Pallas kernels, per_device(): pl.pallas_call(body, name='layer', out_shape=(jax.ShapeDtypeStruct((tok,...  101 us
    unnamed x8, local copies, waits for them, and re-layouts  5.43 us

profile of v1, /device:TPU:9, one launch (start us, length us, event | category | flops | bytes accessed | tf_op | source)
XLA Modules:
  0.0 108.3 jit_solution(9889583960866511787)
XLA Ops:
  0.6 1.3 %jit_solution_.3.refs_4_ = s32[8,256]{1,0:T(8,128)} broadcast(s32[256]{0:T(256)} %constant.2.clone), dimensions={1} | broadcast | bytes 9216 | tf_op jit(solution)
  1.9 100.9 %layer.1 = (bf16[256,512]{1,0:T(8,128)(2,1)}, bf16[256,512]{1,0:T(8,128)(2,1)}, f32[512,512]{1,0:T(8,128)}, f32[512,512]{1,0:T(8,128)}) custom-call(bf16[256,512]{1,0:T(8,128)(2,1)} %bitcast.15, bf16[256,512]{1,0:T(8,128)(2,1)} %bitcast.16, f32[16,16]{1,0:T(8,128)} %refs_2_.1, s32[1,256]{1,0:T(1,128)} %bitcast.17, s32[8,256]{1,0:T(8,128)} %jit_solution_.3.refs_4_, ...), custom_call_target="tpu_custom_call" | custom-call | tf_op jit(solution)/shard_map/layer/pallas_call | solution.py:444
  102.8 0.0 copy-start.1
  102.8 0.0 copy-start
  102.8 1.8 %copy.17 = bf16[16,16,512]{2,1,0:T(8,128)(2,1)} copy(bf16[16,16,512]{2,1,0:T(8,128)(2,1)} %bitcast.14) | data formatting | bytes 524288
  104.6 1.7 %copy.18 = bf16[16,16,512]{2,1,0:T(8,128)(2,1)} copy(bf16[16,16,512]{2,1,0:T(8,128)(2,1)} %bitcast.13) | data formatting | bytes 524288
  106.3 0.0 copy-done.1
  106.3 1.0 copy.19
  107.3 0.0 copy-done
  107.3 1.0 copy.20
Async XLA Ops:
  102.8 3.5 %copy-start.1 = (f32[512,512]{1,0:T(8,128)S(1)}, f32[512,512]{1,0:T(8,128)}, u32[]{:S(2)}) copy-start(f32[512,512]{1,0:T(8,128)} %get-tuple-element.10) | copy-start | bytes 3145732
  102.8 4.5 %copy-start = (f32[512,512]{1,0:T(8,128)S(1)}, f32[512,512]{1,0:T(8,128)}, u32[]{:S(2)}) copy-start(f32[512,512]{1,0:T(8,128)} %get-tuple-element.11) | copy-start | bytes 3145732

commit v2 on v1

--- a/solution.py
+++ b/solution.py
@@ -25,19 +25,26 @@
         self.heights, self.widths = cut(tile_rows), cut(tile_cols)
         self.cells = window_side * window_side
         self.wins, start = [], 0
-        position = np.zeros((tile_rows, tile_cols), np.int32)
-        top = 0
         for i, h in enumerate(self.heights):
-            left = 0
             for j, w in enumerate(self.widths):
-                position[top : top + h, left : left + w] = start + np.arange(h * w).reshape(h, w)
                 sizes = (h * w, (window_side - h) * w, h * (window_side - w), (window_side - h) * (window_side - w))
                 self.wins.append((i, j, start, sizes))
                 start += h * w
-                left += w
-            top += h
-        self.position = position.reshape(-1)
         self.last = (len(self.heights) - 1, len(self.widths) - 1)
+
+    def spots(self, tile_cols, tok):
+        lane = lax.broadcasted_iota(jnp.int32, (1, tok), 1)
+        rows, cols = lane // tile_cols, lax.rem(lane, tile_cols)
+
+        def within(line, sizes):
+            first, size, top = jnp.zeros_like(line), jnp.full_like(line, sizes[0]), 0
+            for before, here in zip(sizes, sizes[1:]):
+                top += before
+                first, size = jnp.where(line >= top, top, first), jnp.where(line >= top, here, size)
+            return first, size
+
+        (top, height), (left, width) = within(rows, self.heights), within(cols, self.widths)
+        return top * tile_cols + left * height + (rows - top) * width + cols - left
 
     def number(self, i, j):
         return i * len(self.widths) + j
@@ -95,7 +102,7 @@
 
 def layer_kernel(
     wins, ring, ranks, cap, tile_cols,
-    tokens, cotangent, gate, route, position, w_qkv_hbm, w_proj_hbm, w_up_hbm, w_down_hbm,
+    tokens, cotangent, gate, route, w_qkv_hbm, w_proj_hbm, w_up_hbm, w_down_hbm,
     layer_out, input_grad, grad_up, grad_down,
     w_qkv, w_proj, w_up, w_down, grouped, ext, kv, queries, context, mixed, upstream, gate_col,
     marks, placers, held, slots, gathered, hidden, pre_grad, parts, back, sums, arrived, share, taken,
@@ -147,7 +154,7 @@
             def _():
                 pl.semaphore_signal(barrier, device_id={"rep": row + v, "exp": me + h})
 
-    spots = position[0:1, :]
+    spots = wins.spots(tile_cols, tok)
     perm = (lax.broadcasted_iota(jnp.int32, (tok, tok), 0) == spots).astype(f32).astype(bf16)
     grouped[...] = dot(perm, tokens[...]).astype(bf16)
     for number, (i, j, start, sizes) in enumerate(wins.wins):
@@ -242,18 +249,17 @@
     make_placer(0)
     dispatch(0, 0, upstream[...])
 
-    def send_weight(index, source, target):
+    def send_weight(index, weight):
         loads[index].wait()
         pltpu.make_async_remote_copy(
-            src_ref=source,
-            dst_ref=target,
+            src_ref=weight.at[0],
+            dst_ref=weight.at[1],
             send_sem=w_send.at[index],
             recv_sem=w_recv.at[index],
             device_id={"rep": buddy},
         ).start()
 
-    send_weight(0, w_up.at[0], w_up.at[1])
-    send_weight(1, w_down.at[0], w_down.at[1])
+    send_weight(0, w_up)
 
     loads[2].wait()
     queries[...] = dot(grouped[...], w_qkv[:, :feature]).astype(bf16)
@@ -300,11 +306,7 @@
         drain(held.at[t, j], z_recv.at[t, j])
         dispatch(t, j, held[t, j])
 
-    count = len(wins.wins)
-    for number in range(count // 2):
-        attend(number)
-    each(1, tiles, lambda j: bring(0, j))
-    for number in range(count // 2, count):
+    for number in range(len(wins.wins)):
         attend(number)
 
     loads[3].wait()
@@ -313,28 +315,29 @@
     mixed[...] = t_dot(perm, blended).astype(bf16)
     each(1, tiles, lambda j: send_tokens(1, mixed, j))
     dispatch(1, 0, mixed[...])
-
-    def arrive(t, j):
-        drain(gathered.at[t, j], a_recv.at[t, j])
+    send_weight(1, w_down)
+    each(1, tiles, lambda j: bring(0, j))
 
     block = min(256, units)
 
-    def experts(j):
-        arrive(0, j)
-        arrive(1, j)
-        for half in range(PAIR):
-            for first in range(0, units, block):
-                spot = pl.ds(half * units + first, block)
-                up, low = w_up[half, pl.ds(first, block), :], w_down[half, pl.ds(first, block), :]
-                pre = dot_t(gathered[1, j], up)
-                flow = dot_t(gathered[0, j], low)
-                square = pre * pre
-                inner = jnp.tanh(GELU_C * (pre + 0.044715 * square * pre))
-                hidden[j, :, spot] = (0.5 * pre * (1.0 + inner)).astype(bf16)
-                slope = 0.5 * (1.0 + inner) + 0.5 * pre * (1.0 - inner * inner) * GELU_C * (
-                    1.0 + 3.0 * 0.044715 * square
-                )
-                pre_grad[j, :, spot] = (flow * slope).astype(bf16)
+    def arrive(j):
+        for t in range(2):
+            drain(gathered.at[t, j], a_recv.at[t, j])
+
+    def stage(j, half):
+        for first in range(0, units, block):
+            spot = pl.ds(half * units + first, block)
+            pre = dot_t(gathered[1, j], w_up[half, pl.ds(first, block), :])
+            flow = dot_t(gathered[0, j], w_down[half, pl.ds(first, block), :])
+            square = pre * pre
+            inner = jnp.tanh(GELU_C * (pre + 0.044715 * square * pre))
+            hidden[j, :, spot] = (0.5 * pre * (1.0 + inner)).astype(bf16)
+            slope = 0.5 * (1.0 + inner) + 0.5 * pre * (1.0 - inner * inner) * GELU_C * (
+                1.0 + 3.0 * 0.044715 * square
+            )
+            pre_grad[j, :, spot] = (flow * slope).astype(bf16)
+
+    def outputs(j):
         for t, (left, right) in enumerate(((hidden, w_down), (pre_grad, w_up))):
             total = dot(left[j, :, pl.ds(0, units)], right[0])
             for half in range(1, PAIR):
@@ -342,11 +345,18 @@
             parts[t, j] = total.astype(bf16)
             swap(parts.at[t, j], back.at[t, j], b_send.at[t, j], b_recv.at[t, j])
 
+    def near_half(j):
+        arrive(j)
+        stage(j, 0)
+
+    near_half(0)
+    each(1, tiles, lambda j: bring(1, j))
+    each(1, tiles, near_half)
     for index, weight in enumerate((w_up, w_down)):
         drain(weight.at[1], w_recv.at[index])
-    experts(0)
-    each(1, tiles, lambda j: bring(1, j))
-    each(1, tiles, experts)
+    each(1, tiles, lambda j: stage(j, 1))
+    each(1, tiles, outputs)
+    stage(0, 1)
 
     rows = tiles * hidden.shape[1]
 
@@ -363,6 +373,8 @@
             recv_sem=g_recv.at[t],
             device_id={"rep": buddy},
         ).start()
+
+    outputs(0)
 
     def placed(t, j):
         drain(back.at[t, j], b_recv.at[t, j])
@@ -424,6 +436,28 @@
     each(1, tiles, finish_far)
 
 
+def store(*values):
+    count = len(values)
+
+    def body(*refs):
+        sems = refs[2 * count]
+        copies = [pltpu.make_async_copy(refs[i], refs[count + i], sems.at[i]) for i in range(count)]
+        for copy in copies:
+            copy.start()
+        for copy in copies:
+            copy.wait()
+
+    return pl.pallas_call(
+        body,
+        name="store",
+        out_shape=tuple(jax.ShapeDtypeStruct(v.shape, v.dtype) for v in values),
+        in_specs=[pl.BlockSpec(memory_space=pltpu.VMEM)] * count,
+        out_specs=(pl.BlockSpec(memory_space=pl.ANY),) * count,
+        scratch_shapes=[pltpu.SemaphoreType.DMA((count,))],
+        compiler_params=pltpu.CompilerParams(vmem_limit_bytes=8 << 20),
+    )(*values)
+
+
 def per_device(ranks, ring, tokens, gate, route, cotangent, w_qkv, w_proj, w_up, w_down):
     tile_rows, tile_cols, feature = tokens.shape
     tok = tile_rows * tile_cols
@@ -434,13 +468,60 @@
     tiles = ranks // PAIR
     wins = Windows(tile_rows, tile_cols)
     ext = len(wins.wins) * wins.cells
-    position = jnp.asarray(np.broadcast_to(wins.position[None, :], (8, tok)))
 
     def body(*refs):
         layer_kernel(wins, ring, ranks, capacity, tile_cols, *refs)
 
-    vmem, anywhere = pl.BlockSpec(memory_space=pltpu.VMEM), pl.BlockSpec(memory_space=pl.ANY)
+    vmem, hbm = pl.BlockSpec(memory_space=pltpu.VMEM), pl.BlockSpec(memory_space=pltpu.HBM)
     dma = pltpu.SemaphoreType.DMA
+    buffers = [
+        pltpu.VMEM(w_qkv.shape, bf16),
+        pltpu.VMEM(w_proj.shape, bf16),
+        pltpu.VMEM((PAIR, units, feature), bf16),
+        pltpu.VMEM((PAIR, units, feature), bf16),
+        pltpu.VMEM((tok, feature), bf16),
+        pltpu.VMEM((ext, feature), bf16),
+        pltpu.VMEM((ext, 2 * feature), bf16),
+        pltpu.VMEM((tok, feature), bf16),
+        pltpu.VMEM((tok, feature), bf16),
+        pltpu.VMEM((tok, feature), bf16),
+        pltpu.VMEM((tok, feature), bf16),
+        pltpu.VMEM((tok, 128), f32),
+        pltpu.VMEM((tiles, 8, tok), jnp.int32),
+        pltpu.VMEM((tiles, rows, tok), bf16),
+        pltpu.VMEM((2, tiles, tok, feature), bf16),
+        pltpu.VMEM((2, tiles, rows, feature), bf16),
+        pltpu.VMEM((2, tiles, rows, feature), bf16),
+        pltpu.VMEM((tiles, rows, PAIR * units), bf16),
+        pltpu.VMEM((tiles, rows, PAIR * units), bf16),
+        pltpu.VMEM((2, tiles, rows, feature), bf16),
+        pltpu.VMEM((2, tiles, rows, feature), bf16),
+        pltpu.VMEM((2, tiles, tok, feature), bf16),
+        pltpu.VMEM((2, tiles, tok, feature), bf16),
+        pltpu.VMEM((2, units, feature), bf16),
+        pltpu.VMEM((2, units, feature), bf16),
+    ]
+    semaphores = [
+        dma((4,)),
+        dma((len(SIDES),)),
+        dma((len(SIDES),)),
+        dma((tiles,)),
+        dma((tiles,)),
+        dma((2, tiles)),
+        dma((2, tiles)),
+        dma((2, tiles)),
+        dma((2, tiles)),
+        dma((2, tiles)),
+        dma((2, tiles)),
+        dma((2,)),
+        dma((2,)),
+        dma((2, tiles)),
+        dma((2, tiles)),
+        dma((2,)),
+        dma((2,)),
+    ]
+    held_bytes = sum(math.prod(ref.shape) * jnp.dtype(ref.dtype).itemsize for ref in buffers)
+    limit = min(60 << 20, held_bytes + (16 << 20))
     layer_out, input_grad, grad_up, grad_down = pl.pallas_call(
         body,
         name="layer",
@@ -450,66 +531,28 @@
             jax.ShapeDtypeStruct((units, feature), f32),
             jax.ShapeDtypeStruct((units, feature), f32),
         ),
-        in_specs=[vmem] * 5 + [anywhere] * 4,
+        in_specs=[vmem] * 4 + [hbm] * 4,
         out_specs=(vmem,) * 4,
-        scratch_shapes=[
-            pltpu.VMEM(w_qkv.shape, bf16),
-            pltpu.VMEM(w_proj.shape, bf16),
-            pltpu.VMEM((PAIR, units, feature), bf16),
-            pltpu.VMEM((PAIR, units, feature), bf16),
-            pltpu.VMEM((tok, feature), bf16),
-            pltpu.VMEM((ext, feature), bf16),
-            pltpu.VMEM((ext, 2 * feature), bf16),
-            pltpu.VMEM((tok, feature), bf16),
-            pltpu.VMEM((tok, feature), bf16),
-            pltpu.VMEM((tok, feature), bf16),
-            pltpu.VMEM((tok, feature), bf16),
-            pltpu.VMEM((tok, 128), f32),
-            pltpu.VMEM((tiles, 8, tok), jnp.int32),
-            pltpu.VMEM((tiles, rows, tok), bf16),
-            pltpu.VMEM((2, tiles, tok, feature), bf16),
-            pltpu.VMEM((2, tiles, rows, feature), bf16),
-            pltpu.VMEM((2, tiles, rows, feature), bf16),
-            pltpu.VMEM((tiles, rows, PAIR * units), bf16),
-            pltpu.VMEM((tiles, rows, PAIR * units), bf16),
-            pltpu.VMEM((2, tiles, rows, feature), bf16),
-            pltpu.VMEM((2, tiles, rows, feature), bf16),
-            pltpu.VMEM((2, tiles, tok, feature), bf16),
-            pltpu.VMEM((2, tiles, tok, feature), bf16),
-            pltpu.VMEM((2, units, feature), bf16),
-            pltpu.VMEM((2, units, feature), bf16),
-            dma((4,)),
-            dma((len(SIDES),)),
-            dma((len(SIDES),)),
-            dma((tiles,)),
-            dma((tiles,)),
-            dma((2, tiles)),
-            dma((2, tiles)),
-            dma((2, tiles)),
-            dma((2, tiles)),
-            dma((2, tiles)),
-            dma((2, tiles)),
-            dma((2,)),
-            dma((2,)),
-            dma((2, tiles)),
-            dma((2, tiles)),
-            dma((2,)),
-            dma((2,)),
-        ],
+        scratch_shapes=buffers + semaphores,
         compiler_params=pltpu.CompilerParams(
-            collective_id=0, has_side_effects=True, vmem_limit_bytes=60 << 20
+            collective_id=0, has_side_effects=True, vmem_limit_bytes=limit
         ),
     )(
-        tokens.reshape(tok, feature),
-        cotangent.reshape(tok, feature),
-        gate,
-        route.reshape(1, tok),
-        position,
-        w_qkv,
-        w_proj,
-        w_up[0],
-        w_down[0],
+        *(
+            pltpu.with_memory_space_constraint(array, pltpu.HBM)
+            for array in (
+                tokens.reshape(tok, feature),
+                cotangent.reshape(tok, feature),
+                gate,
+                route.reshape(1, tok),
+                w_qkv,
+                w_proj,
+                w_up[0],
+                w_down[0],
+            )
+        )
     )
+    layer_out, input_grad, grad_up, grad_down = store(layer_out, input_grad, grad_up, grad_down)
     return (
         layer_out.reshape(tile_rows, tile_cols, feature),
         input_grad.reshape(tile_rows, tile_cols, feature),

time: 108 us -> 85.1 us (0.79)
  the two profiles are of different devices: /device:TPU:9 before, /device:TPU:12 now
where the time goes in v2:
time: 85.1 us; the launch traced here: 85 us
  Pallas kernels  84.3 us (99%)
    pallas_call x1, Pallas kernels, per_device(): pl.pallas_call(body, name='layer', out_shape=(jax.ShapeDtypeStruct((tok,...  82.8 us

profile of v2, /device:TPU:12, one launch (start us, length us, event | category | flops | bytes accessed | tf_op | source)
XLA Modules:
  0.0 85.0 jit_solution(16596955343098077779)
XLA Ops:
  0.6 82.8 %layer.1 = (bf16[256,512]{1,0:T(8,128)(2,1)S(1)}, bf16[256,512]{1,0:T(8,128)(2,1)S(1)}, f32[512,512]{1,0:T(8,128)S(1)}, f32[512,512]{1,0:T(8,128)S(1)}) custom-call(bf16[256,512]{1,0:T(8,128)(2,1)} %bitcast.11, bf16[256,512]{1,0:T(8,128)(2,1)} %bitcast.12, f32[16,16]{1,0:T(8,128)} %refs_2_.1, s32[1,256]{1,0:T(1,128)} %bitcast.13, bf16[512,1536]{1,0:T(8,128)(2,1)} %refs_4_.1, ...), custom_call_target="tpu_custom_call" | custom-call | tf_op jit(solution)/shard_map/layer/pallas_call | solution.py:525
  83.4 1.5 %store.1 = (bf16[256,512]{1,0:T(8,128)(2,1)}, bf16[256,512]{1,0:T(8,128)(2,1)}, f32[512,512]{1,0:T(8,128)}, f32[512,512]{1,0:T(8,128)}) custom-call(bf16[256,512]{1,0:T(8,128)(2,1)S(1)} %get-tuple-element.12.refs_0_, bf16[256,512]{1,0:T(8,128)(2,1)S(1)} %get-tuple-element.13.refs_1_, f32[512,512]{1,0:T(8,128)S(1)} %get-tuple-element.14.refs_2_, ...), custom_call_target="tpu_custom_call" | custom-call | tf_op jit(solution)/shard_map/store/pallas_call | solution.py:450

commit v3 on v2

--- a/solution.py
+++ b/solution.py
@@ -12,6 +12,7 @@
 GELU_C = math.sqrt(2.0 / math.pi)
 window_side = 8
 margin_cells = 4
+WEIGHT_PARTS, AHEAD, EARLY_G, NEARER = 2, 1, True, False
 PAIR = 2
 f32, bf16 = jnp.float32, jnp.bfloat16
 
@@ -67,14 +68,56 @@
         return found
 
 
+class Plan:
+    def __init__(self, ranks, nearer):
+        def handler(tile, pair):
+            low = PAIR * pair
+            if tile // PAIR == pair:
+                return tile
+            return (low if tile < low else low + 1) if nearer else low + tile % PAIR
+
+        handled = [[t for t in range(ranks) if handler(t, p // PAIR) == p] for p in range(ranks)]
+        self.tiles = [sorted(own, key=lambda t, p=p: (abs(t - p), t)) for p, own in enumerate(handled)]
+        self.far = [[p for p in range(ranks) if p != t and t in self.tiles[p]] for t in range(ranks)]
+        self.most = max(len(own) for own in self.tiles)
+        self.sends = max(len(to) for to in self.far)
+        self.counts = sorted({len(own) for own in self.tiles})
+        assert len({len(to) for to in self.far}) == 1
+
+    @staticmethod
+    def pick(row, values):
+        value = values[-1]
+        if len(set(values)) > 1:
+            for rank, other in enumerate(values[:-1]):
+                value = jnp.where(row == rank, other, value)
+        return value
+
+    def handles(self, row, j):
+        flags = [len(own) > j for own in self.tiles]
+        return True if all(flags) else self.pick(row, [int(f) for f in flags]) == 1
+
+    def has(self, row, count):
+        return True if len(self.counts) == 1 else self.pick(row, [len(own) for own in self.tiles]) == count
+
+    def origin(self, row, j):
+        known = [(own[j], self.far[own[j]].index(p)) if len(own) > j else (0, 0) for p, own in enumerate(self.tiles)]
+        return self.pick(row, [t for t, _ in known]), self.pick(row, [k for _, k in known])
+
+    def goal(self, row, k):
+        return (
+            self.pick(row, [to[k] for to in self.far]),
+            self.pick(row, [self.tiles[to[k]].index(t) for t, to in enumerate(self.far)]),
+        )
+
+
+def when(condition, body):
+    if condition is True:
+        body()
+    else:
+        pl.when(condition)(body)
+
+
 SIDES = [(v, h) for v in (-1, 0, 1) for h in (-1, 0, 1) if (v, h) != (0, 0)]
-
-
-def each(begin, end, body):
-    if end - begin == 1:
-        body(begin)
-    elif end > begin:
-        lax.fori_loop(begin, end, lambda k, carry: (body(k), carry)[1], 0)
 
 
 def drain(ref, sem):
@@ -101,31 +144,41 @@
 
 
 def layer_kernel(
-    wins, ring, ranks, cap, tile_cols,
-    tokens, cotangent, gate, route, w_qkv_hbm, w_proj_hbm, w_up_hbm, w_down_hbm,
+    wins, plan, ring, ranks, cap, tile_cols,
+    tokens_hbm, cotangent_hbm, gate_hbm, route_hbm, w_qkv_hbm, w_proj_hbm, w_up_hbm, w_down_hbm,
     layer_out, input_grad, grad_up, grad_down,
-    w_qkv, w_proj, w_up, w_down, grouped, ext, kv, queries, context, mixed, upstream, gate_col,
-    marks, placers, held, slots, gathered, hidden, pre_grad, parts, back, sums, arrived, share, taken,
+    tokens, cotangent, gate, route, w_qkv, w_proj, w_up, w_down, grouped, ext, kv, queries, context, mixed, upstream, gate_col,
+    marks, placers, held, slots, gathered, hidden, slopes, pre_grad, parts, back, sums, arrived, share, taken,
     load_sem, halo_send, halo_recv, mark_send, mark_recv, z_send, z_recv, a_send, a_recv,
     b_send, b_recv, w_send, w_recv, r_send, r_recv, g_send, g_recv,
 ):
     me, row = lax.axis_index("exp"), lax.axis_index("rep")
     tok, feature = tokens.shape
     units = w_up.shape[1]
-    tiles = ranks // PAIR
+    tiles, sends = plan.most, plan.sends
     buddy = row + 1 - 2 * lax.rem(row, 2)
     head_size = feature // HEADS
 
-    def partner(j):
-        return lax.rem(row + PAIR * j, ranks)
-
-    loads = [
-        pltpu.make_async_copy(source, target, load_sem.at[i])
-        for i, (source, target) in enumerate(
-            ((w_up_hbm, w_up.at[0]), (w_down_hbm, w_down.at[0]), (w_qkv_hbm, w_qkv), (w_proj_hbm, w_proj))
+    def others(body):
+        for j in range(1, tiles):
+            when(plan.handles(row, j), lambda j=j: body(j))
+
+    loads = {
+        name: pltpu.make_async_copy(source, target, load_sem.at[i])
+        for i, (name, source, target) in enumerate(
+            (
+                ("tokens", tokens_hbm, tokens),
+                ("route", route_hbm, route),
+                ("gate", gate_hbm, gate),
+                ("cotangent", cotangent_hbm, cotangent),
+                ("up", w_up_hbm, w_up.at[0]),
+                ("qkv", w_qkv_hbm, w_qkv),
+                ("down", w_down_hbm, w_down.at[0]),
+                ("proj", w_proj_hbm, w_proj),
+            )
         )
-    ]
-    for load in loads:
+    }
+    for load in loads.values():
         load.start()
 
     barrier = pltpu.get_barrier_semaphore()
@@ -156,6 +209,7 @@
 
     spots = wins.spots(tile_cols, tok)
     perm = (lax.broadcasted_iota(jnp.int32, (tok, tok), 0) == spots).astype(f32).astype(bf16)
+    loads["tokens"].wait()
     grouped[...] = dot(perm, tokens[...]).astype(bf16)
     for number, (i, j, start, sizes) in enumerate(wins.wins):
         ext[pl.ds(number * wins.cells, sizes[0]), :] = grouped[pl.ds(start, sizes[0]), :]
@@ -183,6 +237,7 @@
                 ).start()
 
     lanes = max(8, ring)
+    loads["route"].wait()
     routes = route[0:1, :].astype(f32)
     match = (lax.broadcasted_iota(jnp.int32, (lanes, tok), 0).astype(f32) == routes).astype(f32)
     before = (
@@ -192,23 +247,27 @@
     ids = routes * cap + jnp.sum(match * earlier, axis=0, keepdims=True)
     marks[0] = jnp.broadcast_to(ids.astype(jnp.int32), marks.shape[1:])
 
-    def send_marks(j):
-        pltpu.make_async_remote_copy(
-            src_ref=marks.at[0],
-            dst_ref=marks.at[tiles - j],
-            send_sem=mark_send.at[j],
-            recv_sem=mark_recv.at[tiles - j],
-            device_id={"rep": partner(j)},
-        ).start()
-
-    def send_tokens(t, source, j):
-        pltpu.make_async_remote_copy(
-            src_ref=source,
-            dst_ref=held.at[t, tiles - j],
-            send_sem=z_send.at[t, j],
-            recv_sem=z_recv.at[t, tiles - j],
-            device_id={"rep": partner(j)},
-        ).start()
+    def send_marks():
+        for k in range(sends):
+            goal, place = plan.goal(row, k)
+            pltpu.make_async_remote_copy(
+                src_ref=marks.at[0],
+                dst_ref=marks.at[place],
+                send_sem=mark_send.at[k],
+                recv_sem=mark_recv.at[place],
+                device_id={"rep": goal},
+            ).start()
+
+    def send_tokens(t, source):
+        for k in range(sends):
+            goal, place = plan.goal(row, k)
+            pltpu.make_async_remote_copy(
+                src_ref=source,
+                dst_ref=held.at[t, place],
+                send_sem=z_send.at[t, k],
+                recv_sem=z_recv.at[t, place],
+                device_id={"rep": goal},
+            ).start()
 
     def make_placer(j):
         slot_ids = lax.broadcasted_iota(jnp.int32, placers.shape[1:], 0)
@@ -235,7 +294,16 @@
         slots[t, j] = dot(placers[j], values).astype(bf16)
         swap(slots.at[t, j], gathered.at[t, j], a_send.at[t, j], a_recv.at[t, j])
 
-    each(1, tiles, send_marks)
+
+    def wait_halo():
+        for index, (v, h) in enumerate(SIDES):
+            @pl.when(near(v, h))
+            def _():
+                amount = sum(rows for _, _, rows in wins.pieces(v, h))
+                drain(grouped.at[pl.ds(0, amount)], halo_recv.at[index])
+
+    loads["gate"].wait()
+    loads["cotangent"].wait()
     grid_row = lax.broadcasted_iota(jnp.int32, (tok, gate.shape[0]), 0) // tile_cols
     picks = (grid_row == lax.broadcasted_iota(jnp.int32, (tok, gate.shape[0]), 1)).astype(f32)
     gate_rows = lax.dot_general(
@@ -245,30 +313,38 @@
     chosen = jnp.where(grid_col == lax.broadcasted_iota(jnp.int32, (tok, tile_cols), 1), gate_rows, 0.0)
     gate_col[...] = jnp.broadcast_to(jnp.sum(chosen, axis=1, keepdims=True), gate_col.shape)
     upstream[...] = (gate_col[:, 0:1] * cotangent[...].astype(f32)).astype(bf16)
-    each(1, tiles, lambda j: send_tokens(0, upstream, j))
     make_placer(0)
+
+    loads["qkv"].wait()
+    queries[...] = dot(grouped[...], w_qkv[:, :feature]).astype(bf16)
+    if not EARLY_G:
+        wait_halo()
+    send_marks()
+    send_tokens(0, upstream)
     dispatch(0, 0, upstream[...])
 
-    def send_weight(index, weight):
-        loads[index].wait()
-        pltpu.make_async_remote_copy(
-            src_ref=weight.at[0],
-            dst_ref=weight.at[1],
-            send_sem=w_send.at[index],
-            recv_sem=w_recv.at[index],
-            device_id={"rep": buddy},
-        ).start()
-
-    send_weight(0, w_up)
-
-    loads[2].wait()
-    queries[...] = dot(grouped[...], w_qkv[:, :feature]).astype(bf16)
-    for index, (v, h) in enumerate(SIDES):
-        @pl.when(near(v, h))
-        def _():
-            amount = sum(rows for _, _, rows in wins.pieces(v, h))
-            drain(grouped.at[pl.ds(0, amount)], halo_recv.at[index])
-
+    chunk = units // WEIGHT_PARTS
+    weights = [(m, p) for m in range(2) for p in range(WEIGHT_PARTS)]
+
+    def weight_part(half, number):
+        m, p = weights[number]
+        return (w_up, w_down)[m].at[half, pl.ds(p * chunk, chunk)]
+
+    def send_weights(numbers):
+        for number in numbers:
+            pltpu.make_async_remote_copy(
+                src_ref=weight_part(0, number),
+                dst_ref=weight_part(1, number),
+                send_sem=w_send.at[number],
+                recv_sem=w_recv.at[number],
+                device_id={"rep": buddy},
+            ).start()
+
+    loads["up"].wait()
+    loads["down"].wait()
+    send_weights(range(AHEAD))
+    if EARLY_G:
+        wait_halo()
     kv[...] = dot(ext[...], w_qkv[:, feature:]).astype(bf16)
     key_lane = lax.broadcasted_iota(jnp.int32, (1, wins.cells), 1)
     group = 128 // head_size
@@ -309,14 +385,14 @@
     for number in range(len(wins.wins)):
         attend(number)
 
-    loads[3].wait()
+    loads["proj"].wait()
     attended = dot(context[...], w_proj[...])
     blended = (grouped[...].astype(f32) + layer_norm(attended)).astype(bf16)
     mixed[...] = t_dot(perm, blended).astype(bf16)
-    each(1, tiles, lambda j: send_tokens(1, mixed, j))
+    send_tokens(1, mixed)
     dispatch(1, 0, mixed[...])
-    send_weight(1, w_down)
-    each(1, tiles, lambda j: bring(0, j))
+    send_weights(range(AHEAD, len(weights)))
+    others(lambda j: bring(0, j))
 
     block = min(256, units)
 
@@ -324,18 +400,21 @@
         for t in range(2):
             drain(gathered.at[t, j], a_recv.at[t, j])
 
-    def stage(j, half):
+    def rise(j, half):
         for first in range(0, units, block):
-            spot = pl.ds(half * units + first, block)
             pre = dot_t(gathered[1, j], w_up[half, pl.ds(first, block), :])
-            flow = dot_t(gathered[0, j], w_down[half, pl.ds(first, block), :])
             square = pre * pre
             inner = jnp.tanh(GELU_C * (pre + 0.044715 * square * pre))
-            hidden[j, :, spot] = (0.5 * pre * (1.0 + inner)).astype(bf16)
-            slope = 0.5 * (1.0 + inner) + 0.5 * pre * (1.0 - inner * inner) * GELU_C * (
+            hidden[j, :, pl.ds(half * units + first, block)] = (0.5 * pre * (1.0 + inner)).astype(bf16)
+            slopes[j, :, pl.ds(first, block)] = 0.5 * (1.0 + inner) + 0.5 * pre * (1.0 - inner * inner) * GELU_C * (
                 1.0 + 3.0 * 0.044715 * square
             )
-            pre_grad[j, :, spot] = (flow * slope).astype(bf16)
+
+    def fall(j, half):
+        for first in range(0, units, block):
+            flow = dot_t(gathered[0, j], w_down[half, pl.ds(first, block), :])
+            spot = pl.ds(half * units + first, block)
+            pre_grad[j, :, spot] = (flow * slopes[j, :, pl.ds(first, block)]).astype(bf16)
 
     def outputs(j):
         for t, (left, right) in enumerate(((hidden, w_down), (pre_grad, w_up))):
@@ -347,25 +426,20 @@
 
     def near_half(j):
         arrive(j)
-        stage(j, 0)
-
-    near_half(0)
-    each(1, tiles, lambda j: bring(1, j))
-    each(1, tiles, near_half)
-    for index, weight in enumerate((w_up, w_down)):
-        drain(weight.at[1], w_recv.at[index])
-    each(1, tiles, lambda j: stage(j, 1))
-    each(1, tiles, outputs)
-    stage(0, 1)
-
-    rows = tiles * hidden.shape[1]
-
-    def gradient(t, half):
-        left = (pre_grad, hidden)[t][...].reshape(rows, PAIR * units)[:, half * units : (half + 1) * units]
-        return t_dot(left, gathered[1 - t].reshape(rows, feature))
-
-    for t in range(2):
-        share[t] = gradient(t, 1).astype(bf16)
+        rise(j, 0)
+        fall(j, 0)
+
+    def gradient(t, half, count):
+        left = (pre_grad, hidden)[t][0:count].reshape(count * hidden.shape[1], PAIR * units)
+        right = gathered[1 - t, 0:count].reshape(count * hidden.shape[1], feature)
+        return t_dot(left[:, half * units : (half + 1) * units], right)
+
+    def give_gradient(t):
+        for count in plan.counts:
+            def partial(count=count):
+                share[t] = gradient(t, 1, count).astype(bf16)
+
+            when(plan.has(row, count), partial)
         pltpu.make_async_remote_copy(
             src_ref=share.at[t],
             dst_ref=taken.at[t],
@@ -374,6 +448,27 @@
             device_id={"rep": buddy},
         ).start()
 
+    def await_weight(m):
+        for number, (matrix, _) in enumerate(weights):
+            if matrix == m:
+                drain(weight_part(1, number), w_recv.at[number])
+
+    near_half(0)
+    others(lambda j: bring(1, j))
+    others(near_half)
+    await_weight(0)
+    rise(0, 1)
+    others(lambda j: rise(j, 1))
+    give_gradient(1)
+    await_weight(1)
+    for j in range(tiles - 1, 0, -1):
+        def far_tile(j=j):
+            fall(j, 1)
+            outputs(j)
+
+        when(plan.handles(row, j), far_tile)
+    fall(0, 1)
+    give_gradient(0)
     outputs(0)
 
     def placed(t, j):
@@ -381,25 +476,31 @@
         return t_dot(placers[j], back[t, j])
 
     def give(j):
+        goal, place = plan.origin(row, j)
         for t in range(2):
             sums[t, j] = placed(t, j).astype(bf16)
             pltpu.make_async_remote_copy(
                 src_ref=sums.at[t, j],
-                dst_ref=arrived.at[t, tiles - j],
+                dst_ref=arrived.at[t, place],
                 send_sem=r_send.at[t, j],
-                recv_sem=r_recv.at[t, tiles - j],
-                device_id={"rep": partner(j)},
+                recv_sem=r_recv.at[t, place],
+                device_id={"rep": goal},
             ).start()
 
-    each(1, tiles, give)
-    grad_up[...] = gradient(0, 0)
-    grad_down[...] = gradient(1, 0)
+    for j in range(tiles - 1, 0, -1):
+        when(plan.handles(row, j), lambda j=j: give(j))
+    for count in plan.counts:
+        def own_gradients(count=count):
+            grad_up[...] = gradient(0, 0, count)
+            grad_down[...] = gradient(1, 0, count)
+
+        when(plan.has(row, count), own_gradients)
 
     def total_of(t):
         value = placed(t, 0)
-        for j in range(1, tiles):
-            drain(arrived.at[t, j], r_recv.at[t, j])
-            value += arrived[t, j].astype(f32)
+        for k in range(sends):
+            drain(arrived.at[t, k], r_recv.at[t, k])
+            value += arrived[t, k].astype(f32)
         return value
 
     layer_out[...] = (mixed[...].astype(f32) + gate_col[:, 0:1] * total_of(0)).astype(bf16)
@@ -415,25 +516,25 @@
             amount = sum(rows for _, _, rows in wins.pieces(-v, -h))
             drain(grouped.at[pl.ds(0, amount)], halo_send.at[index])
 
+    for number in range(len(weights)):
+        drain(weight_part(0, number), w_send.at[number])
     for t in range(2):
-        drain(w_up.at[0], w_send.at[t])
         drain(share.at[t], g_send.at[t])
+        for k in range(sends):
+            drain(mixed, z_send.at[t, k])
+    for k in range(sends):
+        drain(marks.at[0], mark_send.at[k])
 
     def finish(j):
         for t in range(2):
             sent = slots.at[t, j, pl.ds(0, (ring - 1) * cap)]
             drain(sent, a_send.at[t, j])
             drain(sent, b_send.at[t, j])
-
-    each(0, tiles, finish)
-
-    def finish_far(j):
-        drain(marks.at[0], mark_send.at[j])
-        for t in range(2):
-            drain(mixed, z_send.at[t, j])
-            drain(mixed, r_send.at[t, j])
-
-    each(1, tiles, finish_far)
+            if j:
+                drain(mixed, r_send.at[t, j])
+
+    finish(0)
+    others(finish)
 
 
 def store(*values):
@@ -465,63 +566,77 @@
     capacity = max(2, 3 * tok // (2 * ring))
     capacity = -(-capacity // 16) * 16
     rows = ring * capacity
-    tiles = ranks // PAIR
     wins = Windows(tile_rows, tile_cols)
     ext = len(wins.wins) * wins.cells
 
-    def body(*refs):
-        layer_kernel(wins, ring, ranks, capacity, tile_cols, *refs)
-
     vmem, hbm = pl.BlockSpec(memory_space=pltpu.VMEM), pl.BlockSpec(memory_space=pltpu.HBM)
     dma = pltpu.SemaphoreType.DMA
-    buffers = [
-        pltpu.VMEM(w_qkv.shape, bf16),
-        pltpu.VMEM(w_proj.shape, bf16),
-        pltpu.VMEM((PAIR, units, feature), bf16),
-        pltpu.VMEM((PAIR, units, feature), bf16),
-        pltpu.VMEM((tok, feature), bf16),
-        pltpu.VMEM((ext, feature), bf16),
-        pltpu.VMEM((ext, 2 * feature), bf16),
-        pltpu.VMEM((tok, feature), bf16),
-        pltpu.VMEM((tok, feature), bf16),
-        pltpu.VMEM((tok, feature), bf16),
-        pltpu.VMEM((tok, feature), bf16),
-        pltpu.VMEM((tok, 128), f32),
-        pltpu.VMEM((tiles, 8, tok), jnp.int32),
-        pltpu.VMEM((tiles, rows, tok), bf16),
-        pltpu.VMEM((2, tiles, tok, feature), bf16),
-        pltpu.VMEM((2, tiles, rows, feature), bf16),
-        pltpu.VMEM((2, tiles, rows, feature), bf16),
-        pltpu.VMEM((tiles, rows, PAIR * units), bf16),
-        pltpu.VMEM((tiles, rows, PAIR * units), bf16),
-        pltpu.VMEM((2, tiles, rows, feature), bf16),
-        pltpu.VMEM((2, tiles, rows, feature), bf16),
-        pltpu.VMEM((2, tiles, tok, feature), bf16),
-        pltpu.VMEM((2, tiles, tok, feature), bf16),
-        pltpu.VMEM((2, units, feature), bf16),
-        pltpu.VMEM((2, units, feature), bf16),
-    ]
+    def buffers_of(plan):
+        tiles, sends = plan.most, plan.sends
+        return [
+            pltpu.VMEM((tok, feature), bf16),
+            pltpu.VMEM((tok, feature), bf16),
+            pltpu.VMEM(gate.shape, f32),
+            pltpu.VMEM((1, tok), jnp.int32),
+            pltpu.VMEM(w_qkv.shape, bf16),
+            pltpu.VMEM(w_proj.shape, bf16),
+            pltpu.VMEM((PAIR, units, feature), bf16),
+            pltpu.VMEM((PAIR, units, feature), bf16),
+            pltpu.VMEM((tok, feature), bf16),
+            pltpu.VMEM((ext, feature), bf16),
+            pltpu.VMEM((ext, 2 * feature), bf16),
+            pltpu.VMEM((tok, feature), bf16),
+            pltpu.VMEM((tok, feature), bf16),
+            pltpu.VMEM((tok, feature), bf16),
+            pltpu.VMEM((tok, feature), bf16),
+            pltpu.VMEM((tok, 128), f32),
+            pltpu.VMEM((tiles, 8, tok), jnp.int32),
+            pltpu.VMEM((tiles, rows, tok), bf16),
+            pltpu.VMEM((2, tiles, tok, feature), bf16),
+            pltpu.VMEM((2, tiles, rows, feature), bf16),
+            pltpu.VMEM((2, tiles, rows, feature), bf16),
+            pltpu.VMEM((tiles, rows, PAIR * units), bf16),
+            pltpu.VMEM((tiles, rows, units), f32),
+            pltpu.VMEM((tiles, rows, PAIR * units), bf16),
+            pltpu.VMEM((2, tiles, rows, feature), bf16),
+            pltpu.VMEM((2, tiles, rows, feature), bf16),
+            pltpu.VMEM((2, tiles, tok, feature), bf16),
+            pltpu.VMEM((2, max(1, sends), tok, feature), bf16),
+            pltpu.VMEM((2, units, feature), bf16),
+            pltpu.VMEM((2, units, feature), bf16),
+        ]
+
+    def size_of(plan):
+        return sum(math.prod(ref.shape) * jnp.dtype(ref.dtype).itemsize for ref in buffers_of(plan))
+
+    plan = Plan(ranks, NEARER)
+    if size_of(plan) > 44 << 20:
+        plan = Plan(ranks, False)
+    buffers, limit = buffers_of(plan), min(63 << 20, size_of(plan) + (16 << 20))
+    tiles, sends = plan.most, max(1, plan.sends)
     semaphores = [
-        dma((4,)),
+        dma((8,)),
         dma((len(SIDES),)),
         dma((len(SIDES),)),
+        dma((sends,)),
         dma((tiles,)),
-        dma((tiles,)),
+        dma((2, sends)),
         dma((2, tiles)),
         dma((2, tiles)),
         dma((2, tiles)),
         dma((2, tiles)),
         dma((2, tiles)),
+        dma((2 * WEIGHT_PARTS,)),
+        dma((2 * WEIGHT_PARTS,)),
         dma((2, tiles)),
-        dma((2,)),
-        dma((2,)),
-        dma((2, tiles)),
-        dma((2, tiles)),
+        dma((2, sends)),
         dma((2,)),
         dma((2,)),
     ]
-    held_bytes = sum(math.prod(ref.shape) * jnp.dtype(ref.dtype).itemsize for ref in buffers)
-    limit = min(60 << 20, held_bytes + (16 << 20))
+
+    def body(*refs):
+        layer_kernel(wins, plan, ring, ranks, capacity, tile_cols, *refs)
+
     layer_out, input_grad, grad_up, grad_down = pl.pallas_call(
         body,
         name="layer",
@@ -531,7 +646,7 @@
             jax.ShapeDtypeStruct((units, feature), f32),
             jax.ShapeDtypeStruct((units, feature), f32),
         ),
-        in_specs=[vmem] * 4 + [hbm] * 4,
+        in_specs=[hbm] * 8,
         out_specs=(vmem,) * 4,
         scratch_shapes=buffers + semaphores,
         compiler_params=pltpu.CompilerParams(

time: 85.1 us -> 81.3 us (0.955)
  the two profiles are of different devices: /device:TPU:12 before, /device:TPU:7 now
where the time goes in v3:
time: 81.3 us; the launch traced here: 81.2 us
  Pallas kernels  80.5 us (99%)
    pallas_call x1, Pallas kernels, per_device(): pl.pallas_call(body, name='layer', out_shape=(jax.ShapeDtypeStruct((tok,...  79 us

profile of v3, /device:TPU:7, one launch (start us, length us, event | category | flops | bytes accessed | tf_op | source)
XLA Modules:
  0.0 81.2 jit_solution(12918722843661487666)
XLA Ops:
  0.6 79.0 %layer.1 = (bf16[256,512]{1,0:T(8,128)(2,1)S(1)}, bf16[256,512]{1,0:T(8,128)(2,1)S(1)}, f32[512,512]{1,0:T(8,128)S(1)}, f32[512,512]{1,0:T(8,128)S(1)}) custom-call(bf16[256,512]{1,0:T(8,128)(2,1)} %bitcast.11, bf16[256,512]{1,0:T(8,128)(2,1)} %bitcast.12, f32[16,16]{1,0:T(8,128)} %refs_2_.1, s32[1,256]{1,0:T(1,128)} %bitcast.13, bf16[512,1536]{1,0:T(8,128)(2,1)} %refs_4_.1, ...), custom_call_target="tpu_custom_call" | custom-call | tf_op jit(solution)/shard_map/layer/pallas_call | solution.py:640
  79.6 1.5 %store.1 = (bf16[256,512]{1,0:T(8,128)(2,1)}, bf16[256,512]{1,0:T(8,128)(2,1)}, f32[512,512]{1,0:T(8,128)}, f32[512,512]{1,0:T(8,128)}) custom-call(bf16[256,512]{1,0:T(8,128)(2,1)S(1)} %get-tuple-element.12.refs_0_, bf16[256,512]{1,0:T(8,128)(2,1)S(1)} %get-tuple-element.13.refs_1_, f32[512,512]{1,0:T(8,128)S(1)} %get-tuple-element.14.refs_2_, ...), custom_call_target="tpu_custom_call" | custom-call | tf_op jit(solution)/shard_map/store/pallas_call | solution.py:551

commit v4 on v3

--- a/solution.py
+++ b/solution.py
@@ -12,6 +12,7 @@
 GELU_C = math.sqrt(2.0 / math.pi)
 window_side = 8
 margin_cells = 4
+STORE_PARTS = 4
 WEIGHT_PARTS, AHEAD, EARLY_G, NEARER = 2, 1, True, False
 PAIR = 2
 f32, bf16 = jnp.float32, jnp.bfloat16
@@ -461,14 +462,10 @@
     others(lambda j: rise(j, 1))
     give_gradient(1)
     await_weight(1)
-    for j in range(tiles - 1, 0, -1):
-        def far_tile(j=j):
-            fall(j, 1)
-            outputs(j)
-
-        when(plan.handles(row, j), far_tile)
+    others(lambda j: fall(j, 1))
     fall(0, 1)
     give_gradient(0)
+    others(outputs)
     outputs(0)
 
     def placed(t, j):
@@ -503,12 +500,15 @@
             value += arrived[t, k].astype(f32)
         return value
 
+    def finish_gradient(t):
+        drain(taken.at[t], g_recv.at[t])
+        out = (grad_up, grad_down)[t]
+        out[...] = (out[...] + taken[t].astype(f32)) * (1.0 / ranks)
+
+    finish_gradient(1)
     layer_out[...] = (mixed[...].astype(f32) + gate_col[:, 0:1] * total_of(0)).astype(bf16)
     input_grad[...] = total_of(1).astype(bf16)
-    factor = 1.0 / ranks
-    for t, out in enumerate((grad_up, grad_down)):
-        drain(taken.at[t], g_recv.at[t])
-        out[...] = (out[...] + taken[t].astype(f32)) * factor
+    finish_gradient(0)
 
     for index, (v, h) in enumerate(SIDES):
         @pl.when(near(v, h))
@@ -539,10 +539,18 @@
 
 def store(*values):
     count = len(values)
+    pieces = [
+        (i, pl.ds(first, v.shape[0] // STORE_PARTS))
+        for i, v in enumerate(values)
+        for first in range(0, v.shape[0], v.shape[0] // STORE_PARTS)
+    ]
 
     def body(*refs):
         sems = refs[2 * count]
-        copies = [pltpu.make_async_copy(refs[i], refs[count + i], sems.at[i]) for i in range(count)]
+        copies = [
+            pltpu.make_async_copy(refs[i].at[rows], refs[count + i].at[rows], sems.at[n])
+            for n, (i, rows) in enumerate(pieces)
+        ]
         for copy in copies:
             copy.start()
         for copy in copies:
@@ -554,7 +562,7 @@
         out_shape=tuple(jax.ShapeDtypeStruct(v.shape, v.dtype) for v in values),
         in_specs=[pl.BlockSpec(memory_space=pltpu.VMEM)] * count,
         out_specs=(pl.BlockSpec(memory_space=pl.ANY),) * count,
-        scratch_shapes=[pltpu.SemaphoreType.DMA((count,))],
+        scratch_shapes=[pltpu.SemaphoreType.DMA((len(pieces),))],
         compiler_params=pltpu.CompilerParams(vmem_limit_bytes=8 << 20),
     )(*values)
 

time: 81.3 us -> 81.3 us (level)
  no operation moved by 1% of the time
where the time goes in v4:
time: 81.3 us; the launch traced here: 81.1 us
  Pallas kernels  80.5 us (99%)
    pallas_call x1, Pallas kernels, per_device(): pl.pallas_call(body, name='layer', out_shape=(jax.ShapeDtypeStruct((tok,...  78.8 us

profile of v4, /device:TPU:7, one launch (start us, length us, event | category | flops | bytes accessed | tf_op | source)
XLA Modules:
  0.0 81.1 jit_solution(2152465785969052065)
XLA Ops:
  0.6 78.8 %layer.1 = (bf16[256,512]{1,0:T(8,128)(2,1)S(1)}, bf16[256,512]{1,0:T(8,128)(2,1)S(1)}, f32[512,512]{1,0:T(8,128)S(1)}, f32[512,512]{1,0:T(8,128)S(1)}) custom-call(bf16[256,512]{1,0:T(8,128)(2,1)} %bitcast.11, bf16[256,512]{1,0:T(8,128)(2,1)} %bitcast.12, f32[16,16]{1,0:T(8,128)} %refs_2_.1, s32[1,256]{1,0:T(1,128)} %bitcast.13, bf16[512,1536]{1,0:T(8,128)(2,1)} %refs_4_.1, ...), custom_call_target="tpu_custom_call" | custom-call | tf_op jit(solution)/shard_map/layer/pallas_call | solution.py:648
  79.5 1.6 %store.1 = (bf16[256,512]{1,0:T(8,128)(2,1)}, bf16[256,512]{1,0:T(8,128)(2,1)}, f32[512,512]{1,0:T(8,128)}, f32[512,512]{1,0:T(8,128)}) custom-call(bf16[256,512]{1,0:T(8,128)(2,1)S(1)} %get-tuple-element.12.refs_0_, bf16[256,512]{1,0:T(8,128)(2,1)S(1)} %get-tuple-element.13.refs_1_, f32[512,512]{1,0:T(8,128)S(1)} %get-tuple-element.14.refs_2_, ...), custom_call_target="tpu_custom_call" | custom-call | tf_op jit(solution)/shard_map/store/pallas_call | solution.py:559
